TPU v7x, 32 devices: a whole 2x2x4 slice. The times are simulated.
32 devices in a mesh: seq: 16 (over z, x, core), tp: 2 (over y).
Axes of the slice: x: 2, y: 2, z: 4, core: 2. Of those that a mesh axis runs over, the one named last changes fastest.
Arguments:
- tokens: bfloat16 [8192, 3584], P(('seq', 'tp')), may hold values from -6 to 6
- pre_gain: float32 [3584], replicated, may hold values from 0.25 to 1.75
- post_gain: float32 [3584], replicated, may hold values from 0.25 to 1.75
- w_query: bfloat16 [3584, 4096], P('seq', 'tp'), may hold values from -0.09375 to 0.09375
- key_matrix: bfloat16 [3584, 2048], P('seq', 'tp'), may hold values from -0.09375 to 0.09375
- value_matrix: bfloat16 [3584, 2048], P('seq', 'tp'), may hold values from -0.09375 to 0.09375
- w_out: bfloat16 [4096, 3584], P('tp', 'seq'), may hold values from -0.09375 to 0.09375
Outputs:
- block_out: bfloat16 [8192, 3584], P(('seq', 'tp'))
All inputs are finite; a program needn't handle non-finite values.
Results may differ from a plain program's by a relative error of at most 0.014.
Values may be sent and summed in bfloat16 or wider, within the bound.
A program may use at most 128 MiB of HBM per device.

v0:
```python
import jax
import jax.numpy as jnp
from jax import lax
from jax.sharding import PartitionSpec as P

HEAD_SIZE = 256
BLOCK_TOKENS = 512


def from_behind(x, axis, by):
    length = lax.axis_size(axis)
    pairs = [(i, i + by) for i in range(length) if 0 <= i + by < length]
    return lax.ppermute(x, axis, pairs)


def root_norm(values, gain):
    values = values.astype(jnp.float32)
    return values * lax.rsqrt(jnp.mean(values * values, axis=-1, keepdims=True) + 1e-06) * gain


def rotate_halves(values, token_positions):
    row_count = values.shape[0]
    shaped = values.reshape(row_count, -1, HEAD_SIZE)
    half_dim = HEAD_SIZE // 2
    freq = 10000.0 ** (-(jnp.arange(half_dim).astype(jnp.float32) * 2.0 / HEAD_SIZE))
    angle = token_positions[:, None] * freq[None, :]
    cosine = jnp.cos(angle)[:, None, :]
    sine_part = jnp.sin(angle)[:, None, :]
    first = shaped[..., :half_dim]
    second = shaped[..., half_dim:]
    turned = jnp.concatenate(
        [first * cosine - second * sine_part, second * cosine + first * sine_part], axis=-1
    )
    return turned.reshape(row_count, -1)


def attend(query_rows, keys_now, vals_now, keys_prior, vals_prior, offset_pos):
    length = query_rows.shape[0]
    kv_heads = keys_now.shape[1] // HEAD_SIZE
    repeat_heads = query_rows.shape[1] // (HEAD_SIZE * kv_heads)
    query_grouped = query_rows.reshape(length, kv_heads, repeat_heads, HEAD_SIZE)
    key_current = jnp.concatenate([keys_prior, keys_now], axis=0).reshape(
        2 * length, kv_heads, HEAD_SIZE
    )
    value_current = jnp.concatenate([vals_prior, vals_now], axis=0).reshape(
        2 * length, kv_heads, HEAD_SIZE
    )
    attention_scores = jnp.einsum(
        "cwap,bwp->wacb", query_grouped, key_current, preferred_element_type=jnp.float32
    )
    query_idx = jnp.arange(length)[:, None]
    key_idx = jnp.arange(2 * length)[None, :]
    key_pos = offset_pos - length + key_idx
    allowed = (key_idx > query_idx) & (key_idx <= query_idx + length) & (key_pos >= 0)
    weights = jnp.where(allowed, jnp.exp(attention_scores), 0.0)
    denominator = jnp.sum(weights, axis=-1)
    weight_narrow = weights.astype(jnp.bfloat16)
    reduced_output = jnp.einsum(
        "bpqu,ubm->qbpm", weight_narrow, value_current, preferred_element_type=jnp.float32
    )
    attended = reduced_output / jnp.transpose(denominator, (2, 0, 1))[..., None]
    return attended.astype(jnp.bfloat16).reshape(length, -1)


def local(tokens, pre_gain, post_gain, w_query, key_matrix, value_matrix, w_out):
    normalized_input = root_norm(tokens, pre_gain).astype(jnp.bfloat16)
    gathered = lax.all_gather(normalized_input, "tp", axis=0, tiled=True)
    pieces = (
        lax.all_gather(w_query, "seq", axis=0, tiled=True),
        lax.all_gather(key_matrix, "seq", axis=0, tiled=True),
        lax.all_gather(value_matrix, "seq", axis=0, tiled=True),
    )
    raw_q, raw_k, raw_v = tuple(
        (jnp.dot(gathered, piece, preferred_element_type=jnp.float32) for piece in pieces)
    )
    offset_pos = lax.axis_index("seq") * BLOCK_TOKENS
    token_positions = (offset_pos + jnp.arange(BLOCK_TOKENS)).astype(jnp.float32)
    query_rows = (rotate_halves(raw_q, token_positions) * HEAD_SIZE ** (-0.5)).astype(jnp.bfloat16)
    keys_now = rotate_halves(raw_k, token_positions).astype(jnp.bfloat16)
    vals_now = raw_v.astype(jnp.bfloat16)
    keys_prior, vals_prior = from_behind((keys_now, vals_now), "seq", 1)
    attended = attend(query_rows, keys_now, vals_now, keys_prior, vals_prior, offset_pos)
    partial_value = jnp.dot(
        attended,
        lax.all_gather(w_out, "seq", axis=1, tiled=True),
        preferred_element_type=jnp.float32,
    )
    own_rows = lax.psum_scatter(
        partial_value.astype(jnp.bfloat16), "tp", scatter_dimension=0, tiled=True
    ).astype(jnp.float32)
    mixed = root_norm(own_rows, post_gain)
    return (tokens.astype(jnp.float32) + mixed).astype(jnp.bfloat16)


def solution(mesh):
    return jax.shard_map(
        local,
        mesh=mesh,
        in_specs=(
            P(("seq", "tp"), None),
            P(),
            P(),
            P("seq", "tp"),
            P("seq", "tp"),
            P("seq", "tp"),
            P("tp", "seq"),
        ),
        out_specs=P(("seq", "tp"), None),
        check_vma=False,
    )
```

profile of v0, /device:TPU:0, one launch (start us, length us, event | category | flops | bytes accessed | tf_op | source)
XLA Modules:
  0.0 518.1 jit_solution(9972426617604793397)
XLA Ops:
  6.5 1.9 fusion.10
  8.5 3.2 fusion.12
  15.5 50.0 %all-gather.6.cloned.1.call-done = bf16[512,3584]{1,0:T(8,128)(2,1)} async-done(((bf16[256,3584]{1,0:T(8,128)(2,1)}), bf16[512,3584]{1,0:T(8,128)(2,1)}) %all-gather.6.cloned.1.call-update) | async-done | bytes 3670032 | tf_op jit(solution)/shard_map/all_gather | solution.py:67
  65.5 70.0 %all-gather.8.cloned.1.call-done = bf16[3584,1024]{1,0:T(8,128)(2,1)} async-done(((bf16[224,1024]{1,0:T(8,128)(2,1)}), bf16[3584,1024]{1,0:T(8,128)(2,1)}) %all-gather.8.cloned.1.call-update) | async-done | bytes 7340048 | tf_op jit(solution)/shard_map/all_gather | solution.py:71
  135.4 9.1 %convolution_convert_fusion.1 = bf16[512,1024]{1,0:T(8,128)(2,1)} fusion(bf16[512,3584]{1,0:T(8,128)(2,1)} %all-gather.6.cloned.1.call-done, bf16[3584,1024]{1,0:T(8,128)(2,1)} %all-gather.8.cloned.1.call-done), kind=kOutput, calls=%fused_computation.30 | convolution fusion | flops 3758620672 | bytes 12058624 | tf_op jit(solution)/shard_map/dot_general | solution.py:74
  144.6 3.2 collective-permute-start
  147.7 60.8 %all-gather.10.cloned.1.call-done = bf16[3584,1024]{1,0:T(8,128)(2,1)} async-done(((bf16[224,1024]{1,0:T(8,128)(2,1)}), bf16[3584,1024]{1,0:T(8,128)(2,1)}) %all-gather.10.cloned.1.call-update) | async-done | bytes 7340048 | tf_op jit(solution)/shard_map/all_gather | solution.py:70
  208.5 9.5 %fusion.19 = f32[512,1024]{1,0:T(8,128)} fusion(bf16[512,3584]{1,0:T(8,128)(2,1)} %all-gather.6.cloned.1.call-done, bf16[3584,1024]{1,0:T(8,128)(2,1)} %all-gather.10.cloned.1.call-done), kind=kOutput, calls=%fused_computation.43 | convolution fusion | flops 3758096384 | bytes 13107200 | tf_op jit(solution)/shard_map/dot_general | solution.py:74
  218.0 2.2 reshape.114
  222.4 3.1 collective-permute-start.1
  225.5 1.3 fusion.17
  226.8 1.7 pad_maximum_fusion
  228.5 2.8 copy.19
  231.2 1.5 pad_maximum_fusion.1
  232.8 99.3 %all-gather.12.cloned.1.call-done = bf16[3584,2048]{1,0:T(8,128)(2,1)} async-done(((bf16[224,2048]{1,0:T(8,128)(2,1)}), bf16[3584,2048]{1,0:T(8,128)(2,1)}) %all-gather.12.cloned.1.call-update) | async-done | bytes 14680080 | tf_op jit(solution)/shard_map/all_gather | solution.py:69
  332.1 12.1 %fusion.20 = f32[512,2048]{1,0:T(8,128)S(1)} fusion(bf16[512,3584]{1,0:T(8,128)(2,1)} %all-gather.6.cloned.1.call-done, bf16[3584,2048]{1,0:T(8,128)(2,1)} %all-gather.12.cloned.1.call-done), kind=kOutput, calls=%fused_computation.44 | convolution fusion | flops 7516192768 | bytes 22544384 | tf_op jit(solution)/shard_map/dot_general | solution.py:74
  344.2 2.0 copy.22
  348.2 8.3 %fusion = (f32[4,2,512]{2,1,0:T(2,128)S(1)}, f32[4,1024,512,2]{2,1,3,0:T(8,128)}) fusion(pred[512,1024]{0,1:T(8,128)(4,1)S(1)} %copy-done.4, bf16[1024,4,256,1]{0,2,3,1:T(8,128)(2,1)S(1)} %bitcast.45, bf16[512,4,2,256]{3,0,2,1:T(8,128)(2,1)S(1)} %bitcast.46), kind=kOutput, calls=%fused_computation.1 | convolution fusion | flops 2155868160 | bytes 21512192 | tf_op jit(solution)/shard_map/cwap,bwp->wacb/dot_general | solution.py:48
  356.5 8.7 %fusion.7 = bf16[512,4,2,256]{0,3,2,1:T(8,128)(2,1)S(1)} fusion(bf16[1024,4,256,1]{0,2,3,1:T(8,128)(2,1)S(1)} %bitcast.44, f32[4,1024,512,2]{2,1,3,0:T(8,128)} %get-tuple-element.12, pred[512,1024]{0,1:T(8,128)(4,1)S(1)} %copy-done.4, f32[512,4,2]{0,2,1:T(2,128)S(1)} %bitcast.48), kind=kOutput, calls=%fused_computation.15 | convolution fusion | flops 2157969408 | bytes 21512192 | tf_op jit(solution)/shard_map/bpqu,ubm->qbpm/dot_general | solution.py:58
  365.2 80.6 %all-gather.14.cloned.1.call-done = bf16[2048,3584]{0,1:T(8,128)(2,1)} async-done(((bf16[2048,224]{0,1:T(8,128)(2,1)}), bf16[2048,3584]{0,1:T(8,128)(2,1)}) %all-gather.14.cloned.1.call-update) | async-done | bytes 14680080 | tf_op jit(solution)/shard_map/all_gather | solution.py:85
  445.8 12.4 %convolution_convert_fusion = bf16[512,3584]{1,0:T(8,128)(2,1)} fusion(bf16[512,2048]{0,1:T(8,128)(2,1)S(1)} %bitcast.47, bf16[2048,3584]{0,1:T(8,128)(2,1)} %all-gather.14.cloned.1.call-done), kind=kOutput, calls=%fused_computation.6 | convolution fusion | flops 7518027776 | bytes 20447232 | tf_op jit(solution)/shard_map/dot_general | solution.py:83
  458.2 47.5 %reduce-scatter.2.cloned.1.call-done = bf16[256,3584]{1,0:T(8,128)(2,1)} async-done(((bf16[512,3584]{1,0:T(8,128)(2,1)}), bf16[256,3584]{1,0:T(8,128)(2,1)}) %reduce-scatter.2.cloned.1.call-update) | async-done | bytes 1835024 | tf_op jit(solution)/shard_map/reduce_scatter | solution.py:88
  505.7 1.9 fusion.8
  507.7 3.6 fusion.13
  (39 shorter events, 7.8 us)
Async XLA Ops:
  6.5 58.9 %all-gather.6.cloned.1.call-start = ((), (), s32[]{:S(2)}) async-start(), calls=%async_computation.1 | async-start | bytes 5505024 | tf_op jit(solution)/shard_map/all_gather | solution.py:67
  11.8 123.7 %all-gather.8.cloned.1.call-start = ((), (), s32[]{:S(2)}) async-start(), calls=%async_computation.2 | async-start | bytes 7798784 | tf_op jit(solution)/shard_map/all_gather | solution.py:71
  12.5 196.0 %all-gather.10.cloned.1.call-start = ((), (), s32[]{:S(2)}) async-start(), calls=%async_computation.3 | async-start | bytes 7798784 | tf_op jit(solution)/shard_map/all_gather | solution.py:70
  13.2 318.9 %all-gather.12.cloned.1.call-start = ((), (), s32[]{:S(2)}) async-start(), calls=%async_computation.4 | async-start | bytes 15597568 | tf_op jit(solution)/shard_map/all_gather | solution.py:69
  13.8 432.0 %all-gather.14.cloned.1.call-start = ((), (), s32[]{:S(2)}) async-start(), calls=%async_computation.5 | async-start | bytes 15597568 | tf_op jit(solution)/shard_map/all_gather | solution.py:85
  14.4 491.3 %reduce-scatter.2.cloned.1.call-start = ((), (), s32[]{:S(2)}) async-start(), calls=%async_computation.6 | async-start | bytes 5505024 | tf_op jit(solution)/shard_map/reduce_scatter | solution.py:88
  15.5 204.8 %copy-start.1 = (f32[512,128]{1,0:T(8,128)}, f32[512,128]{1,0:T(8,128)S(1)}, u32[]{:S(2)}) copy-start(f32[512,128]{1,0:T(8,128)S(1)} %get-tuple-element.10) | copy-start | bytes 786436
  144.6 82.2 %collective-permute-start = (bf16[512,1024]{1,0:T(8,128)(2,1)}, bf16[512,1024]{1,0:T(8,128)(2,1)}, u32[]{:S(2)}, u32[]{:S(2)}) collective-permute-start(bf16[512,1024]{1,0:T(8,128)(2,1)} %convolution_convert_fusion.1), channel_id=1, source_target_pairs={{0,2},{2,4},{4,6},{6,8},{8,10},{10,12},{12,14},{14,16},{16,18},{18... | collective-permute-start | bytes 3145736 | tf_op jit(solution)/shard_map/ppermute | solution.py:13
  222.4 8.9 %collective-permute-start.1 = (bf16[512,1024]{0,1:T(8,128)(2,1)S(1)}, bf16[512,1024]{0,1:T(8,128)(2,1)}, u32[]{:S(2)}, u32[]{:S(2)}) collective-permute-start(bf16[512,1024]{0,1:T(8,128)(2,1)S(1)} %bitcast.42), channel_id=1, source_target_pairs={{0,2},{2,4},{4,6},{6,8},{8,10},{10,12},{12,14},{14,16},{16,18},{18... | collective-permute-start | bytes 3145736 | tf_op jit(solution)/shard_map/ppermute | solution.py:13
  344.2 2.0 copy-start.2
  347.2 1.0 copy-start.4
  348.2 8.3 %copy-start.3 = (bf16[1024,1024]{0,1:T(8,128)(2,1)S(1)}, bf16[1024,1024]{0,1:T(8,128)(2,1)}, u32[]{:S(2)}) copy-start(bf16[1024,1024]{0,1:T(8,128)(2,1)} %copy.19) | copy-start | bytes 6291460
  458.2 49.5 %copy-start = (bf16[256,3584]{1,0:T(8,128)(2,1)S(1)}, bf16[256,3584]{1,0:T(8,128)(2,1)}, u32[]{:S(2)}) copy-start(bf16[256,3584]{1,0:T(8,128)(2,1)} %param.7) | copy-start | bytes 5505028
  458.2 49.5 %copy-start.5 = (f32[3584]{0:T(1024)S(1)}, f32[3584]{0:T(1024)}, u32[]{:S(2)}) copy-start(f32[3584]{0:T(1024)} %param.9) | copy-start | bytes 43012
Sparse Core Ops, SparseCore 0:
  11.9 53.5 all-gather.5
  67.7 67.6 all-gather.7
  137.7 70.7 all-gather.9
  210.7 121.4 all-gather.11
  334.3 111.4 all-gather.13
  458.4 47.3 reduce-scatter.1
where the time goes:
time: 519 us; the launch traced here: 518 us
  waiting for transfers between devices  411 us (79%)
  matrix products  60 us (12%)
  other arithmetic  18.3 us (4%)
  between operations  13.6 us (3%)
  local copies, waits for them, and re-layouts  8.96 us (2%)
  starting transfers between devices  6.47 us (1%)
    all_gather x1, waiting for transfers between devices, local(): lax.all_gather(w_query, 'seq', axis=0, tiled=True)  99.3 us
    all_gather x1, waiting for transfers between devices, local(): lax.all_gather(w_out, 'seq', axis=1, tiled=True)  80.6 us
    all_gather x1, waiting for transfers between devices, local(): lax.all_gather(value_matrix, 'seq', axis=0, tiled=True)  70 us
    all_gather x1, waiting for transfers between devices, local(): lax.all_gather(key_matrix, 'seq', axis=0, tiled=True)  60.8 us
    all_gather x1, waiting for transfers between devices, local(): gathered = lax.all_gather(normalized_input, 'tp', axis=0, tiled=True)  50 us
    reduce_scatter x1, waiting for transfers between devices, local(): lax.psum_scatter(partial_value.astype(jnp.bfloat16), 'tp', scatter_dimens...  47.5 us
    dot_general x3, matrix products, local(): jnp.dot(gathered, piece, preferred_element_type=jnp.float32)  30.7 us
    dot_general x1, matrix products, local(): jnp.dot(attended, lax.all_gather(w_out, 'seq', axis=1, tiled=True), prefe...  12.4 us
  transfers between devices with their start and end apart: 8, of which 6 were waited for; matrix products, arithmetic and copies ran while one was open for 12% of the time, Pallas kernels for 0%

commit v1 on v0

--- a/solution.py
+++ b/solution.py
@@ -4,13 +4,21 @@
 from jax.sharding import PartitionSpec as P
 
 HEAD_SIZE = 256
-BLOCK_TOKENS = 512
+PLANE = 4
 
 
 def from_behind(x, axis, by):
     length = lax.axis_size(axis)
     pairs = [(i, i + by) for i in range(length) if 0 <= i + by < length]
     return lax.ppermute(x, axis, pairs)
+
+
+def swap_seq(x, bits):
+    return lax.ppermute(x, "seq", [(i, i ^ bits) for i in range(lax.axis_size("seq"))])
+
+
+def swap_tp(x):
+    return lax.ppermute(x, "tp", [(0, 1), (1, 0)])
 
 
 def root_norm(values, gain):
@@ -62,7 +70,147 @@
     return attended.astype(jnp.bfloat16).reshape(length, -1)
 
 
+def line_gather(piece, plane, planes):
+    up = [(i, i + PLANE) for i in range(PLANE * (planes - 1))]
+    down = [(i + PLANE, i) for i in range(PLANE * (planes - 1))]
+    from_below, from_above = [piece], [piece]
+    for _ in range(planes - 1):
+        from_below.append(lax.ppermute(from_below[-1], "seq", up))
+        from_above.append(lax.ppermute(from_above[-1], "seq", down))
+    return [piece] + [
+        jnp.where(plane + k < planes, from_above[k], from_below[planes - k])
+        for k in range(1, planes)
+    ]
+
+
+def cyclic(x, begin, axis):
+    return lax.dynamic_slice_in_dim(
+        jnp.concatenate([x, x], axis=axis), begin, x.shape[axis], axis
+    )
+
+
+def attend_positions(queries, keys, vals, query_pos, key_pos, window):
+    scores = jnp.einsum("bqhd,bkd->bhqk", queries, keys, preferred_element_type=jnp.float32)
+    gap = query_pos[:, :, None] - key_pos[:, None, :]
+    allowed = (gap >= 0) & (gap < window) & (key_pos[:, None, :] >= 0)
+    weights = jnp.where(allowed[:, None], jnp.exp(scores), 0.0)
+    denominator = jnp.sum(weights, axis=-1)
+    mixed = jnp.einsum(
+        "bhqk,bkd->bqhd", weights.astype(jnp.bfloat16), vals, preferred_element_type=jnp.float32
+    )
+    return (mixed / jnp.transpose(denominator, (0, 2, 1))[..., None]).astype(jnp.bfloat16)
+
+
+def scatter_add(part, bits_first):
+    def along_x(v):
+        return v[0] + swap_seq(v[1].astype(jnp.bfloat16), 2).astype(jnp.float32)
+
+    def along_y(v):
+        return v[0] + swap_tp(v[1].astype(jnp.bfloat16)).astype(jnp.float32)
+
+    if bits_first == "x":
+        return along_y(along_x(part))
+    return along_x(along_y(jnp.swapaxes(part, 0, 1)))
+
+
+def local_plane(tokens, pre_gain, post_gain, w_query, key_matrix, value_matrix, w_out):
+    seq = lax.axis_index("seq")
+    n_seq = lax.axis_size("seq")
+    planes = n_seq // PLANE
+    plane = seq // PLANE
+    tp = lax.axis_index("tp")
+    own_rows, width = tokens.shape
+    block = own_rows * lax.axis_size("tp")
+    groups = [list(range(PLANE * i, PLANE * (i + 1))) for i in range(planes)]
+
+    def trade(w, split_axis, concat_axis):
+        return lax.all_to_all(
+            w, "seq", split_axis=split_axis, concat_axis=concat_axis, tiled=True,
+            axis_index_groups=groups,
+        )
+
+    depth = key_matrix.shape[0]
+    kv = jnp.concatenate(
+        [key_matrix.reshape(depth, PLANE, -1), value_matrix.reshape(depth, PLANE, -1)], axis=2
+    ).reshape(depth, -1)
+    w_kv = jnp.concatenate(line_gather(trade(kv, 1, 0), plane, planes), axis=0)
+    w_q = jnp.concatenate(line_gather(trade(w_query, 1, 0), plane, planes), axis=0)
+    out_piece = trade(w_out, 0, 1)
+    span = out_piece.shape[1]
+    cut = -(-span // 256) * 128
+    w_o = [line_gather(out_piece[:, :cut], plane, planes), line_gather(out_piece[:, cut:], plane, planes)]
+
+    normed = root_norm(tokens, pre_gain).astype(jnp.bfloat16)
+    own = cyclic(normed, plane * span, 1)
+    over_y = swap_tp(own)
+    over_x = swap_seq(own, 2)
+    half = own_rows // 2
+    far = jnp.concatenate([swap_seq(over_y[:half], 2), swap_tp(over_x[half:])], axis=0)
+    near_rows = jnp.concatenate([own, over_y, over_x, far], axis=0)
+    far_rows = swap_seq(near_rows, 1)
+
+    flips = [(dc + 2 * dx, dy) for dc in (0, 1) for dx in (0, 1) for dy in (0, 1)]
+    begins = [(seq ^ s) * block + (tp ^ t) * own_rows for s, t in flips]
+    positions = jnp.concatenate([b + jnp.arange(own_rows) for b in begins])
+    float_pos = positions.astype(jnp.float32)
+
+    raw_kv = jnp.concatenate(
+        [jnp.dot(r, w_kv, preferred_element_type=jnp.float32) for r in (near_rows, far_rows)], axis=0
+    )
+    kv_width = raw_kv.shape[1] // 2
+    keys = rotate_halves(raw_kv[:, :kv_width], float_pos).astype(jnp.bfloat16)
+    kv_rows = jnp.concatenate([keys, raw_kv[:, kv_width:].astype(jnp.bfloat16)], axis=1)
+    plane_rows = PLANE * block
+    ordered = jnp.zeros((plane_rows, 2 * kv_width), jnp.bfloat16)
+    for i, b in enumerate(begins):
+        ordered = lax.dynamic_update_slice_in_dim(
+            ordered, kv_rows[i * own_rows : (i + 1) * own_rows], b - plane * plane_rows, 0
+        )
+    prior = from_behind(ordered[plane_rows - block :], "seq", PLANE)
+    window = jnp.concatenate([prior, ordered], axis=0)
+
+    raw_q = jnp.concatenate(
+        [jnp.dot(r, w_q, preferred_element_type=jnp.float32) for r in (near_rows, far_rows)], axis=0
+    )
+    queries = (rotate_halves(raw_q, float_pos) * HEAD_SIZE ** (-0.5)).astype(jnp.bfloat16)
+    firsts = [seq ^ s for s in range(PLANE)]
+    firsts = [firsts[0], firsts[2], firsts[1], firsts[3]]
+    seen = jnp.stack(
+        [
+            lax.dynamic_slice_in_dim(window, (f - plane * PLANE) * block, 2 * block, 0)
+            for f in firsts
+        ]
+    )
+    key_pos = jnp.stack([(f - 1) * block + jnp.arange(2 * block) for f in firsts])
+    attended = attend_positions(
+        queries.reshape(PLANE, block, -1, HEAD_SIZE),
+        seen[..., :kv_width],
+        seen[..., kv_width:],
+        positions.reshape(PLANE, block),
+        key_pos,
+        block,
+    ).reshape(plane_rows, -1)
+
+    sums = []
+    for pieces in w_o:
+        weights = jnp.concatenate(pieces, axis=1)
+        theirs = jnp.dot(attended[plane_rows // 2 :], weights, preferred_element_type=jnp.float32)
+        theirs = swap_seq(theirs.astype(jnp.bfloat16), 1)
+        part = jnp.dot(attended[: plane_rows // 2], weights, preferred_element_type=jnp.float32)
+        part = (part + theirs.astype(jnp.float32)).reshape(2, 2, own_rows, -1)
+        middle = part.shape[3] // 2
+        total = jnp.concatenate(
+            [scatter_add(part[..., :middle], "x"), scatter_add(part[..., middle:], "y")], axis=1
+        )
+        sums.append(total.reshape(own_rows, planes, -1))
+    projected = jnp.concatenate(sums, axis=2).reshape(own_rows, width)
+    projected = cyclic(projected, (planes - plane) % planes * span, 1)
+    mixed = root_norm(projected, post_gain)
+    return (tokens.astype(jnp.float32) + mixed).astype(jnp.bfloat16)
+
+
 def local(tokens, pre_gain, post_gain, w_query, key_matrix, value_matrix, w_out):
+    block = tokens.shape[0] * lax.axis_size("tp")
     normalized_input = root_norm(tokens, pre_gain).astype(jnp.bfloat16)
     gathered = lax.all_gather(normalized_input, "tp", axis=0, tiled=True)
     pieces = (
@@ -73,8 +221,8 @@
     raw_q, raw_k, raw_v = tuple(
         (jnp.dot(gathered, piece, preferred_element_type=jnp.float32) for piece in pieces)
     )
-    offset_pos = lax.axis_index("seq") * BLOCK_TOKENS
-    token_positions = (offset_pos + jnp.arange(BLOCK_TOKENS)).astype(jnp.float32)
+    offset_pos = lax.axis_index("seq") * block
+    token_positions = (offset_pos + jnp.arange(block)).astype(jnp.float32)
     query_rows = (rotate_halves(raw_q, token_positions) * HEAD_SIZE ** (-0.5)).astype(jnp.bfloat16)
     keys_now = rotate_halves(raw_k, token_positions).astype(jnp.bfloat16)
     vals_now = raw_v.astype(jnp.bfloat16)
@@ -93,8 +241,13 @@
 
 
 def solution(mesh):
+    def body(*args):
+        kv_heads = args[4].shape[1] // HEAD_SIZE
+        by_plane = kv_heads % PLANE == 0 and mesh.shape["seq"] % PLANE == 0 and mesh.shape["tp"] == 2
+        return (local_plane if by_plane else local)(*args)
+
     return jax.shard_map(
-        local,
+        body,
         mesh=mesh,
         in_specs=(
             P(("seq", "tp"), None),

time: 519 us -> 477 us (0.919); the launches traced: 518 us -> 468 us
  waiting for transfers between devices: 411 us -> 202 us
  starting transfers between devices: 6.47 us -> 100 us
  other arithmetic: 18.3 us -> 56.7 us
  local copies, waits for them, and re-layouts: 8.96 us -> 45.8 us
  between operations: 13.6 us -> 1.55 us
    all_gather x5 -> x0, waiting for transfers between devices: 361 us -> none  [the longest x1 99.3 us: local(): lax.all_gather(w_query, 'seq', axis=0, tiled=True)]
    ppermute x0 -> x39, waiting for transfers between devices: none -> 162 us  [the longest x12 69.7 us: line_gather(): from_above.append(lax.ppermute(from_above[-1], 'seq', down))]
    ppermute x0 -> x39, starting transfers between devices: none -> 83.9 us  [the longest x12 52.7 us: line_gather(): from_below.append(lax.ppermute(from_below[-1], 'seq', up))]
    reduce_scatter x1 -> x0, waiting for transfers between devices: 47.5 us -> none  [local(): lax.psum_scatter(partial_value.astype(jnp.bfloat16), 'tp', scatter_dimens...]
    all_to_all x0 -> x3, waiting for transfers between devices: none -> 39.3 us  [trade(): lax.all_to_all(w, 'seq', split_axis=split_axis, concat_axis=concat_axis,...]
    select_n x0 -> x12, other arithmetic: none -> 12.1 us  [line_gather(): jnp.where(plane + k < planes, from_above[k], from_below[planes - k])]
    all_to_all x0 -> x3, starting transfers between devices: none -> 11.2 us  [trade(): lax.all_to_all(w, 'seq', split_axis=split_axis, concat_axis=concat_axis,...]
    slice x0 -> x9, local copies, waits for them, and re-layouts: none -> 9.18 us  [the longest x2 2.64 us: local_plane(): attended[:plane_rows // 2]]
  transfers between devices with their start and end apart: 8 -> 43, of which waited for: 6 -> 19; matrix products, arithmetic and copies ran while one was open for 12% -> 30% of each run, Pallas kernels for 0% -> 0%
where the time goes in v1:
time: 477 us; the launch traced here: 468 us
  waiting for transfers between devices  202 us (42%)
  starting transfers between devices  100 us (21%)
  matrix products  62.2 us (13%)
  other arithmetic  56.7 us (12%)
  local copies, waits for them, and re-layouts  45.8 us (10%)
    ppermute x12, waiting for transfers between devices, line_gather(): from_above.append(lax.ppermute(from_above[-1], 'seq', down))  69.7 us
    ppermute x9, waiting for transfers between devices, swap_seq(): lax.ppermute(x, 'seq', [(i, i ^ bits) for i in range(lax.axis_size('seq'))])  55.7 us
    ppermute x12, starting transfers between devices, line_gather(): from_below.append(lax.ppermute(from_below[-1], 'seq', up))  52.7 us
    all_to_all x3, waiting for transfers between devices, trade(): lax.all_to_all(w, 'seq', split_axis=split_axis, concat_axis=concat_axis,...  39.3 us
    ppermute x12, waiting for transfers between devices, line_gather(): from_below.append(lax.ppermute(from_below[-1], 'seq', up))  30.8 us
    ppermute x12, starting transfers between devices, line_gather(): from_above.append(lax.ppermute(from_above[-1], 'seq', down))  16.1 us
    dot_general x2, matrix products, local_plane(): jnp.dot(r, w_kv, preferred_element_type=jnp.float32)  12.3 us
    select_n x12, other arithmetic, line_gather(): jnp.where(plane + k < planes, from_above[k], from_below[planes - k])  12.1 us
  transfers between devices with their start and end apart: 43, of which 19 were waited for; matrix products, arithmetic and copies ran while one was open for 30% of the time, Pallas kernels for 0%

profile of v1, /device:TPU:0, one launch (start us, length us, event | category | flops | bytes accessed | tf_op | source)
XLA Modules:
  0.0 468.2 jit_solution(14988233920054653181)
XLA Ops:
  23.8 37.2 %all-to-all-done.2 = bf16[4,512,224]{1,2,0:T(8,128)(2,1)S(1)} async-done(((bf16[4,512,224]{1,2,0:T(8,128)(2,1)}), bf16[4,512,224]{1,2,0:T(8,128)(2,1)S(1)}, u32[]{:S(2)}, u32[]{:S(2)}) %all-to-all-start.2) | async-done | bytes 917536 | tf_op jit(solution)/shard_map/all_to_all | solution.py:127
  71.0 5.4 %collective-permute-start.19 = (bf16[512,512]{0,1:T(8,128)(2,1)S(1)}, bf16[512,512]{0,1:T(8,128)(2,1)}, u32[]{:S(2)}, u32[]{:S(2)}) collective-permute-start(bf16[512,512]{0,1:T(8,128)(2,1)S(1)} %slice.215), channel_id=1, source_target_pairs={{0,8},{2,10},{4,12},{6,14},{8,16},{10,18},{12,20},{14,22},{16,24},... | collective-permute-start | bytes 1572872 | tf_op jit(solution)/shard_map/ppermute | solution.py:78
  84.6 13.8 %collective-permute-done.2 = bf16[128,3584]{1,0:T(8,128)(2,1)S(1)} collective-permute-done((bf16[128,3584]{1,0:T(8,128)(2,1)S(1)}, bf16[128,3584]{1,0:T(8,128)(2,1)S(1)}, u32[]{:S(2)}, u32[]{:S(2)}) %collective-permute-start.2) | collective-permute-done | bytes 917536 | tf_op jit(solution)/shard_map/ppermute | solution.py:17
  118.6 18.6 %collective-permute-done.31 = bf16[512,384]{0,1:T(8,128)(2,1)S(1)} collective-permute-done((bf16[512,384]{0,1:T(8,128)(2,1)S(1)}, bf16[512,384]{0,1:T(8,128)(2,1)S(1)}, u32[]{:S(2)}, u32[]{:S(2)}) %collective-permute-start.31) | collective-permute-done | bytes 393248 | tf_op jit(solution)/shard_map/ppermute | solution.py:78
  144.3 4.8 %collective-permute-start.32 = (bf16[512,384]{0,1:T(8,128)(2,1)}, bf16[512,384]{0,1:T(8,128)(2,1)S(1)}, u32[]{:S(2)}, u32[]{:S(2)}) collective-permute-start(bf16[512,384]{0,1:T(8,128)(2,1)} %copy-done.27), channel_id=1, source_target_pairs={{0,8},{2,10},{4,12},{6,14},{8,16},{10,18},{12,20},{14,22},{16,24},... | collective-permute-start | bytes 1179656 | tf_op jit(solution)/shard_map/ppermute | solution.py:78
  154.6 8.4 %collective-permute-done.13 = bf16[896,512]{1,0:T(8,128)(2,1)S(1)} collective-permute-done((bf16[896,512]{1,0:T(8,128)(2,1)S(1)}, bf16[896,512]{1,0:T(8,128)(2,1)S(1)}, u32[]{:S(2)}, u32[]{:S(2)}) %collective-permute-start.13) | collective-permute-done | bytes 917536 | tf_op jit(solution)/shard_map/ppermute | solution.py:78
  167.8 4.9 %collective-permute-start.6 = (bf16[896,512]{1,0:T(8,128)(2,1)}, bf16[896,512]{1,0:T(8,128)(2,1)}, u32[]{:S(2)}, u32[]{:S(2)}) collective-permute-start(bf16[896,512]{1,0:T(8,128)(2,1)} %collective-permute-done.5), channel_id=1, source_target_pairs={{0,8},{2,10},{4,12},{6,14},{8,16},{10,18},{12,20},{14,22},{16,24},... | collective-permute-start | bytes 2752520 | tf_op jit(solution)/shard_map/ppermute | solution.py:78
  174.8 6.0 %multiply_cosine_fusion = (f32[2048,128]{1,0:T(8,128)S(1)}, f32[2048,128]{1,0:T(8,128)}) fusion(f32[128]{0:T(128)} %negate_power_fusion, f32[2048]{0:T(1024)S(1)} %convert_element_type.115), kind=kLoop, calls=%fused_computation.90 | loop fusion | flops 262144 | bytes 2105856 | tf_op jit(solution)/shard_map/cos | solution.py:35
  180.8 15.2 %collective-permute-done.34 = bf16[512,384]{0,1:T(8,128)(2,1)} collective-permute-done((bf16[512,384]{0,1:T(8,128)(2,1)}, bf16[512,384]{0,1:T(8,128)(2,1)}, u32[]{:S(2)}, u32[]{:S(2)}) %collective-permute-start.34) | collective-permute-done | bytes 393248 | tf_op jit(solution)/shard_map/ppermute | solution.py:79
  222.2 13.0 %collective-permute-done.9 = bf16[896,512]{1,0:T(8,128)(2,1)S(1)} collective-permute-done((bf16[896,512]{1,0:T(8,128)(2,1)}, bf16[896,512]{1,0:T(8,128)(2,1)S(1)}, u32[]{:S(2)}, u32[]{:S(2)}) %collective-permute-start.9) | collective-permute-done | bytes 917536 | tf_op jit(solution)/shard_map/ppermute | solution.py:79
  240.6 24.3 %collective-permute-done.18 = bf16[512,512]{0,1:T(8,128)(2,1)} collective-permute-done((bf16[512,512]{0,1:T(8,128)(2,1)S(1)}, bf16[512,512]{0,1:T(8,128)(2,1)}, u32[]{:S(2)}, u32[]{:S(2)}) %collective-permute-start.18) | collective-permute-done | bytes 524320 | tf_op jit(solution)/shard_map/ppermute | solution.py:79
  272.8 5.1 %fusion.54 = f32[1024,512]{1,0:T(8,128)S(1)} fusion(bf16[1024,3584]{1,0:T(8,128)(2,1)S(1)} %bitcast.156, bf16[896,512]{1,0:T(8,128)(2,1)S(1)} %broadcast_select_fusion.1, bf16[896,512]{1,0:T(8,128)(2,1)S(1)} %broadcast_select_fusion.3, bf16[896,512]{1,0:T(8,128)(2,1)S(1)} %broadcast_select_fusion.5, bf16[896,512]{1,0:T(8,128)(2,1)} %bitcast.1), kind=kOutput, calls=%fused_computation.138 | convolution fusion | flops 3772776448 | bytes 13107200 | tf_op jit(solution)/shard_map/dot_general | solution.py:158
  281.9 7.2 %fusion.53 = f32[1024,512]{1,0:T(8,128)S(1)} fusion(bf16[1024,3584]{1,0:T(8,128)(2,1)} %collective-permute-done.10, bf16[896,512]{1,0:T(8,128)(2,1)S(1)} %broadcast_select_fusion.1, bf16[896,512]{1,0:T(8,128)(2,1)S(1)} %broadcast_select_fusion.3, bf16[896,512]{1,0:T(8,128)(2,1)S(1)} %broadcast_select_fusion.5, bf16[896,512]{1,0:T(8,128)(2,1)} %bitcast.1), kind=kOutput, calls=%fused_computation.137 | convolution fusion | flops 3772776448 | bytes 13107200 | tf_op jit(solution)/shard_map/dot_general | solution.py:158
  289.9 4.7 fusion.32
  296.0 5.3 %collective-permute-start.11 = (bf16[512,512]{1,0:T(8,128)(2,1)}, bf16[512,512]{1,0:T(8,128)(2,1)}, u32[]{:S(2)}, u32[]{:S(2)}) collective-permute-start(bf16[512,512]{1,0:T(8,128)(2,1)} %slice.209), channel_id=1, source_target_pairs={{0,8},{2,10},{4,12},{6,14},{8,16},{10,18},{12,20},{14,22},{16,24},... | collective-permute-start | bytes 1572872 | tf_op jit(solution)/shard_map/ppermute | solution.py:13
  301.3 7.0 %fusion.51 = f32[1024,512]{1,0:T(8,128)S(1)} fusion(bf16[1024,3584]{1,0:T(8,128)(2,1)} %collective-permute-done.10, bf16[896,512]{1,0:T(8,128)(2,1)S(1)} %broadcast_select_fusion, bf16[896,512]{1,0:T(8,128)(2,1)S(1)} %broadcast_select_fusion.2, bf16[896,512]{1,0:T(8,128)(2,1)S(1)} %broadcast_select_fusion.4, bf16[896,512]{1,0:T(8,128)(2,1)S(1)} %bitcast.154), kind=kOutput, calls=%fused_computation.135 | convolution fusion | flops 3772776448 | bytes 13107200 | tf_op jit(solution)/shard_map/dot_general | solution.py:173
  310.8 6.1 %reshape.289 = f32[2048,2,256]{2,1,0:T(2,128)} reshape(f32[2048,512]{1,0:T(8,128)} %pad_maximum_fusion.1) | data formatting | bytes 8388608 | tf_op jit(solution)/shard_map/reshape | solution.py:31
  325.9 7.9 %fusion = (f32[4,2,512]{2,1,0:T(2,128)S(1)}, f32[4,1024,512,2]{2,1,3,0:T(8,128)}) fusion(pred[4,512,1024]{1,2,0:T(8,128)(4,1)S(1)} %copy-done.5, bf16[4,512,2,256]{3,1,0,2:T(8,128)(2,1)S(1)} %bitcast.144, bf16[4,1024,512]{2,1,0:T(8,128)(2,1)S(1)} %pad_maximum_fusion), kind=kOutput, calls=%fused_computation.1 | convolution fusion | flops 2155868160 | bytes 23085056 | tf_op jit(solution)/shard_map/bqhd,bkd->bhqk/dot_general | solution.py:93
  333.8 10.8 %fusion.9 = bf16[4,512,2,256]{1,3,2,0:T(8,128)(2,1)} fusion(f32[4,1024,512,2]{2,1,3,0:T(8,128)} %get-tuple-element.24, pred[4,512,1024]{1,2,0:T(8,128)(4,1)S(1)} %copy-done.5, bf16[4,1024,512]{2,1,0:T(8,128)(2,1)S(1)} %pad_maximum_fusion, f32[4,512,2]{1,2,0:T(2,128)S(1)} %bitcast.157), kind=kOutput, calls=%fused_computation.29 | convolution fusion | flops 2157969408 | bytes 23085056 | tf_op jit(solution)/shard_map/bhqk,bkd->bqhd/dot_general | solution.py:98
  347.8 4.7 %convolution_convert_fusion = bf16[1024,1536]{1,0:T(8,128)(2,1)} fusion(bf16[1024,512]{1,0:T(8,128)(2,1)S(1)} %bitcast.147, bf16[512,384]{0,1:T(8,128)(2,1)} %broadcast_select_fusion.9, bf16[512,384]{0,1:T(8,128)(2,1)S(1)} %copy-done.25, bf16[512,384]{0,1:T(8,128)(2,1)} %broadcast_select_fusion.11, bf16[512,384]{0,1:T(8,128)(2,1)} %slice.226), kind=kOutput, calls=%fused_computation.30 | convolution fusion | flops 1618477056 | bytes 5767168 | tf_op jit(solution)/shard_map/dot_general | solution.py:197
  359.7 9.3 %collective-permute-done.23 = bf16[512,512]{0,1:T(8,128)(2,1)S(1)} collective-permute-done((bf16[512,512]{0,1:T(8,128)(2,1)}, bf16[512,512]{0,1:T(8,128)(2,1)S(1)}, u32[]{:S(2)}, u32[]{:S(2)}) %collective-permute-start.23) | collective-permute-done | bytes 524320 | tf_op jit(solution)/shard_map/ppermute | solution.py:79
  385.6 17.0 %collective-permute-done.36 = bf16[2,256,768]{2,1,0:T(8,128)(2,1)} collective-permute-done((bf16[2,256,768]{2,1,0:T(8,128)(2,1)}, bf16[2,256,768]{2,1,0:T(8,128)(2,1)}, u32[]{:S(2)}, u32[]{:S(2)}) %collective-permute-start.36) | collective-permute-done | bytes 786464 | tf_op jit(solution)/shard_map/ppermute | solution.py:17
  408.0 6.8 %convert_add_fusion = f32[1024,2048]{1,0:T(8,128)S(1)} fusion(bf16[1024,2048]{1,0:T(8,128)(2,1)} %collective-permute-done.24, bf16[1024,512]{1,0:T(8,128)(2,1)S(1)} %bitcast.146, bf16[512,512]{0,1:T(8,128)(2,1)S(1)} %copy-done.20, bf16[512,512]{0,1:T(8,128)(2,1)S(1)} %copy-done.18, bf16[512,512]{0,1:T(8,128)(2,1)S(1)} %copy-done.22, ...), kind=kOutput, calls=%fused_computation.6 | convolution fusion | flops 2160066560 | bytes 15728640 | tf_op jit(solution)/shard_map/dot_general | solution.py:199
  417.8 22.0 %collective-permute-done.25 = bf16[2,256,1024]{2,1,0:T(8,128)(2,1)S(1)} collective-permute-done((bf16[2,256,1024]{2,1,0:T(8,128)(2,1)S(1)}, bf16[2,256,1024]{2,1,0:T(8,128)(2,1)S(1)}, u32[]{:S(2)}, u32[]{:S(2)}) %collective-permute-start.25) | collective-permute-done | bytes 1048608 | tf_op jit(solution)/shard_map/ppermute | solution.py:17
  (241 shorter events, 201.0 us)
Async XLA Ops:
  6.5 69.8 %collective-permute-start = (bf16[256,3584]{1,0:T(8,128)(2,1)}, bf16[256,3584]{1,0:T(8,128)(2,1)S(1)}, u32[]{:S(2)}, u32[]{:S(2)}) collective-permute-start(bf16[256,3584]{1,0:T(8,128)(2,1)} %get-tuple-element.8), channel_id=1, source_target_pairs={{0,1},{1,0},{2,3},{3,2},{4,5},{5,4},{6,7},{7,6},{8,9},{9,8},{10,11... | collective-permute-start | bytes 5505032 | tf_op jit(solution)/shard_map/ppermute | solution.py:21
  9.5 69.0 %collective-permute-start.1 = (bf16[256,3584]{1,0:T(8,128)(2,1)}, bf16[256,3584]{1,0:T(8,128)(2,1)}, u32[]{:S(2)}, u32[]{:S(2)}) collective-permute-start(bf16[256,3584]{1,0:T(8,128)(2,1)} %get-tuple-element.8), channel_id=1, source_target_pairs={{0,4},{2,6},{4,0},{6,2},{8,12},{10,14},{12,8},{14,10},{16,20},{18,... | collective-permute-start | bytes 5505032 | tf_op jit(solution)/shard_map/ppermute | solution.py:17
  12.0 49.0 %all-to-all-start.2 = ((bf16[4,512,224]{1,2,0:T(8,128)(2,1)}), bf16[4,512,224]{1,2,0:T(8,128)(2,1)S(1)}, u32[]{:S(2)}, u32[]{:S(2)}) async-start(bf16[4,512,224]{1,2,0:T(8,128)(2,1)} %bitcast.143), calls=%async_computation.2 | async-start | bytes 1835008 | tf_op jit(solution)/shard_map/all_to_all | solution.py:127
  61.1 41.0 %all-to-all-start = ((bf16[224,4,512]{2,0,1:T(8,128)(2,1)}), bf16[224,4,512]{2,0,1:T(8,128)(2,1)}, u32[]{:S(2)}, u32[]{:S(2)}) async-start(bf16[224,4,512]{2,0,1:T(8,128)(2,1)} %copy.33), calls=%async_computation | async-start | bytes 1835008 | tf_op jit(solution)/shard_map/all_to_all | solution.py:127
  66.2 43.0 %collective-permute-start.30 = (bf16[512,384]{0,1:T(8,128)(2,1)}, bf16[512,384]{0,1:T(8,128)(2,1)S(1)}, u32[]{:S(2)}, u32[]{:S(2)}) collective-permute-start(bf16[512,384]{0,1:T(8,128)(2,1)} %slice.226), channel_id=1, source_target_pairs={{0,8},{2,10},{4,12},{6,14},{8,16},{10,18},{12,20},{14,22},{16,24},... | collective-permute-start | bytes 1179656 | tf_op jit(solution)/shard_map/ppermute | solution.py:78
  69.7 40.8 %collective-permute-start.29 = (bf16[512,384]{0,1:T(8,128)(2,1)}, bf16[512,384]{0,1:T(8,128)(2,1)}, u32[]{:S(2)}, u32[]{:S(2)}) collective-permute-start(bf16[512,384]{0,1:T(8,128)(2,1)} %slice.226), channel_id=1, source_target_pairs={{8,0},{10,2},{12,4},{14,6},{16,8},{18,10},{20,12},{22,14},{24,16},... | collective-permute-start | bytes 1179656 | tf_op jit(solution)/shard_map/ppermute | solution.py:79
  71.0 44.1 %collective-permute-start.19 = (bf16[512,512]{0,1:T(8,128)(2,1)S(1)}, bf16[512,512]{0,1:T(8,128)(2,1)}, u32[]{:S(2)}, u32[]{:S(2)}) collective-permute-start(bf16[512,512]{0,1:T(8,128)(2,1)S(1)} %slice.215), channel_id=1, source_target_pairs={{0,8},{2,10},{4,12},{6,14},{8,16},{10,18},{12,20},{14,22},{16,24},... | collective-permute-start | bytes 1572872 | tf_op jit(solution)/shard_map/ppermute | solution.py:78
  102.1 179.8 %collective-permute-start.10 = (bf16[1024,3584]{1,0:T(8,128)(2,1)}, bf16[1024,3584]{1,0:T(8,128)(2,1)}, u32[]{:S(2)}, u32[]{:S(2)}) collective-permute-start(bf16[1024,3584]{1,0:T(8,128)(2,1)} %constant_dynamic-update-slice_fusion), channel_id=1, source_target_pairs={{0,2},{2,0},{4,6},{6,4},{8,10},{10,8},{12,14},{14,12},{16,18},{18,... | collective-permute-start | bytes 22020104 | tf_op jit(solution)/shard_map/ppermute | solution.py:17
  105.6 38.7 %collective-permute-start.5 = (bf16[896,512]{1,0:T(8,128)(2,1)}, bf16[896,512]{1,0:T(8,128)(2,1)}, u32[]{:S(2)}, u32[]{:S(2)}) collective-permute-start(bf16[896,512]{1,0:T(8,128)(2,1)} %bitcast.1), channel_id=1, source_target_pairs={{0,8},{2,10},{4,12},{6,14},{8,16},{10,18},{12,20},{14,22},{16,24},... | collective-permute-start | bytes 2752520 | tf_op jit(solution)/shard_map/ppermute | solution.py:78
  109.2 39.9 %collective-permute-start.4 = (bf16[896,512]{1,0:T(8,128)(2,1)}, bf16[896,512]{1,0:T(8,128)(2,1)S(1)}, u32[]{:S(2)}, u32[]{:S(2)}) collective-permute-start(bf16[896,512]{1,0:T(8,128)(2,1)} %bitcast.1), channel_id=1, source_target_pairs={{8,0},{10,2},{12,4},{14,6},{16,8},{18,10},{20,12},{22,14},{24,16},... | collective-permute-start | bytes 2752520 | tf_op jit(solution)/shard_map/ppermute | solution.py:79
  115.1 27.2 %collective-permute-start.33 = (bf16[512,384]{0,1:T(8,128)(2,1)}, bf16[512,384]{0,1:T(8,128)(2,1)}, u32[]{:S(2)}, u32[]{:S(2)}) collective-permute-start(bf16[512,384]{0,1:T(8,128)(2,1)} %collective-permute-done.29), channel_id=1, source_target_pairs={{8,0},{10,2},{12,4},{14,6},{16,8},{18,10},{20,12},{22,14},{24,16},... | collective-permute-start | bytes 1179656 | tf_op jit(solution)/shard_map/ppermute | solution.py:79
  144.3 28.5 %collective-permute-start.32 = (bf16[512,384]{0,1:T(8,128)(2,1)}, bf16[512,384]{0,1:T(8,128)(2,1)S(1)}, u32[]{:S(2)}, u32[]{:S(2)}) collective-permute-start(bf16[512,384]{0,1:T(8,128)(2,1)} %copy-done.27), channel_id=1, source_target_pairs={{0,8},{2,10},{4,12},{6,14},{8,16},{10,18},{12,20},{14,22},{16,24},... | collective-permute-start | bytes 1179656 | tf_op jit(solution)/shard_map/ppermute | solution.py:78
  149.1 50.8 %collective-permute-start.8 = (bf16[896,512]{1,0:T(8,128)(2,1)S(1)}, bf16[896,512]{1,0:T(8,128)(2,1)}, u32[]{:S(2)}, u32[]{:S(2)}) collective-permute-start(bf16[896,512]{1,0:T(8,128)(2,1)S(1)} %collective-permute-done.4), channel_id=1, source_target_pairs={{8,0},{10,2},{12,4},{14,6},{16,8},{18,10},{20,12},{22,14},{24,16},... | collective-permute-start | bytes 2752520 | tf_op jit(solution)/shard_map/ppermute | solution.py:79
  163.0 32.9 %collective-permute-start.34 = (bf16[512,384]{0,1:T(8,128)(2,1)}, bf16[512,384]{0,1:T(8,128)(2,1)}, u32[]{:S(2)}, u32[]{:S(2)}) collective-permute-start(bf16[512,384]{0,1:T(8,128)(2,1)} %collective-permute-done.33), channel_id=1, source_target_pairs={{8,0},{10,2},{12,4},{14,6},{16,8},{18,10},{20,12},{22,14},{24,16},... | collective-permute-start | bytes 1179656 | tf_op jit(solution)/shard_map/ppermute | solution.py:79
  167.8 37.0 %collective-permute-start.6 = (bf16[896,512]{1,0:T(8,128)(2,1)}, bf16[896,512]{1,0:T(8,128)(2,1)}, u32[]{:S(2)}, u32[]{:S(2)}) collective-permute-start(bf16[896,512]{1,0:T(8,128)(2,1)} %collective-permute-done.5), channel_id=1, source_target_pairs={{0,8},{2,10},{4,12},{6,14},{8,16},{10,18},{12,20},{14,22},{16,24},... | collective-permute-start | bytes 2752520 | tf_op jit(solution)/shard_map/ppermute | solution.py:78
  173.5 42.1 %collective-permute-start.16 = (bf16[896,512]{1,0:T(8,128)(2,1)}, bf16[896,512]{1,0:T(8,128)(2,1)}, u32[]{:S(2)}, u32[]{:S(2)}) collective-permute-start(bf16[896,512]{1,0:T(8,128)(2,1)} %collective-permute-done.12), channel_id=1, source_target_pairs={{8,0},{10,2},{12,4},{14,6},{16,8},{18,10},{20,12},{22,14},{24,16},... | collective-permute-start | bytes 2752520 | tf_op jit(solution)/shard_map/ppermute | solution.py:79
  199.9 35.2 %collective-permute-start.9 = (bf16[896,512]{1,0:T(8,128)(2,1)}, bf16[896,512]{1,0:T(8,128)(2,1)S(1)}, u32[]{:S(2)}, u32[]{:S(2)}) collective-permute-start(bf16[896,512]{1,0:T(8,128)(2,1)} %collective-permute-done.8), channel_id=1, source_target_pairs={{8,0},{10,2},{12,4},{14,6},{16,8},{18,10},{20,12},{22,14},{24,16},... | collective-permute-start | bytes 2752520 | tf_op jit(solution)/shard_map/ppermute | solution.py:79
  204.8 64.5 %collective-permute-start.7 = (bf16[896,512]{1,0:T(8,128)(2,1)}, bf16[896,512]{1,0:T(8,128)(2,1)S(1)}, u32[]{:S(2)}, u32[]{:S(2)}) collective-permute-start(bf16[896,512]{1,0:T(8,128)(2,1)} %collective-permute-done.6), channel_id=1, source_target_pairs={{0,8},{2,10},{4,12},{6,14},{8,16},{10,18},{12,20},{14,22},{16,24},... | collective-permute-start | bytes 2752520 | tf_op jit(solution)/shard_map/ppermute | solution.py:78
  215.6 55.7 %collective-permute-start.17 = (bf16[896,512]{1,0:T(8,128)(2,1)}, bf16[896,512]{1,0:T(8,128)(2,1)S(1)}, u32[]{:S(2)}, u32[]{:S(2)}) collective-permute-start(bf16[896,512]{1,0:T(8,128)(2,1)} %collective-permute-done.16), channel_id=1, source_target_pairs={{8,0},{10,2},{12,4},{14,6},{16,8},{18,10},{20,12},{22,14},{24,16},... | collective-permute-start | bytes 2752520 | tf_op jit(solution)/shard_map/ppermute | solution.py:79
  220.9 44.0 %collective-permute-start.18 = (bf16[512,512]{0,1:T(8,128)(2,1)S(1)}, bf16[512,512]{0,1:T(8,128)(2,1)}, u32[]{:S(2)}, u32[]{:S(2)}) collective-permute-start(bf16[512,512]{0,1:T(8,128)(2,1)S(1)} %copy-done.14), channel_id=1, source_target_pairs={{8,0},{10,2},{12,4},{14,6},{16,8},{18,10},{20,12},{22,14},{24,16},... | collective-permute-start | bytes 1572872 | tf_op jit(solution)/shard_map/ppermute | solution.py:79
  235.2 36.3 %collective-permute-start.15 = (bf16[896,512]{1,0:T(8,128)(2,1)S(1)}, bf16[896,512]{1,0:T(8,128)(2,1)S(1)}, u32[]{:S(2)}, u32[]{:S(2)}) collective-permute-start(bf16[896,512]{1,0:T(8,128)(2,1)S(1)} %collective-permute-done.14), channel_id=1, source_target_pairs={{0,8},{2,10},{4,12},{6,14},{8,16},{10,18},{12,20},{14,22},{16,24},... | collective-permute-start | bytes 2752520 | tf_op jit(solution)/shard_map/ppermute | solution.py:78
  264.9 89.1 %collective-permute-start.20 = (bf16[512,512]{0,1:T(8,128)(2,1)}, bf16[512,512]{0,1:T(8,128)(2,1)}, u32[]{:S(2)}, u32[]{:S(2)}) collective-permute-start(bf16[512,512]{0,1:T(8,128)(2,1)} %collective-permute-done.19), channel_id=1, source_target_pairs={{0,8},{2,10},{4,12},{6,14},{8,16},{10,18},{12,20},{14,22},{16,24},... | collective-permute-start | bytes 1572872 | tf_op jit(solution)/shard_map/ppermute | solution.py:78
  269.4 83.2 %collective-permute-start.22 = (bf16[512,512]{0,1:T(8,128)(2,1)}, bf16[512,512]{0,1:T(8,128)(2,1)}, u32[]{:S(2)}, u32[]{:S(2)}) collective-permute-start(bf16[512,512]{0,1:T(8,128)(2,1)} %collective-permute-done.18), channel_id=1, source_target_pairs={{8,0},{10,2},{12,4},{14,6},{16,8},{18,10},{20,12},{22,14},{24,16},... | collective-permute-start | bytes 1572872 | tf_op jit(solution)/shard_map/ppermute | solution.py:79
  375.8 32.2 %collective-permute-start.24 = (bf16[1024,2048]{1,0:T(8,128)(2,1)}, bf16[1024,2048]{1,0:T(8,128)(2,1)}, u32[]{:S(2)}, u32[]{:S(2)}) collective-permute-start(bf16[1024,2048]{1,0:T(8,128)(2,1)} %convolution_convert_fusion.1), channel_id=1, source_target_pairs={{0,2},{2,0},{4,6},{6,4},{8,10},{10,8},{12,14},{14,12},{16,18},{18,... | collective-permute-start | bytes 12582920 | tf_op jit(solution)/shard_map/ppermute | solution.py:17
  (53 other events, 921.4 us)

commit v2 on v1

--- a/solution.py
+++ b/solution.py
@@ -70,16 +70,28 @@
     return attended.astype(jnp.bfloat16).reshape(length, -1)
 
 
-def line_gather(piece, plane, planes):
-    up = [(i, i + PLANE) for i in range(PLANE * (planes - 1))]
-    down = [(i + PLANE, i) for i in range(PLANE * (planes - 1))]
-    from_below, from_above = [piece], [piece]
-    for _ in range(planes - 1):
-        from_below.append(lax.ppermute(from_below[-1], "seq", up))
-        from_above.append(lax.ppermute(from_above[-1], "seq", down))
-    return [piece] + [
-        jnp.where(plane + k < planes, from_above[k], from_below[planes - k])
-        for k in range(1, planes)
+def hop(line):
+    below, above = line
+    devices = lax.axis_size("seq") - PLANE
+    up = [(i, i + PLANE) for i in range(devices)]
+    down = [(i + PLANE, i) for i in range(devices)]
+    return (
+        below + [lax.ppermute(below[-1], "seq", up)],
+        above + [lax.ppermute(above[-1], "seq", down)],
+    )
+
+
+def hold(line, *others):
+    below, above = line
+    newest, *others = lax.optimization_barrier(((below[-1], above[-1]), *others))
+    return (below[:-1] + [newest[0]], above[:-1] + [newest[1]]), *others
+
+
+def line_pieces(line, plane):
+    below, above = line
+    planes = len(below)
+    return [below[0]] + [
+        jnp.where(plane + k < planes, above[k], below[planes - k]) for k in range(1, planes)
     ]
 
 
@@ -133,30 +145,46 @@
     kv = jnp.concatenate(
         [key_matrix.reshape(depth, PLANE, -1), value_matrix.reshape(depth, PLANE, -1)], axis=2
     ).reshape(depth, -1)
-    w_kv = jnp.concatenate(line_gather(trade(kv, 1, 0), plane, planes), axis=0)
-    w_q = jnp.concatenate(line_gather(trade(w_query, 1, 0), plane, planes), axis=0)
+    inner_hops = planes - 3
+
+    kv_piece = trade(kv, 1, 0)
+    w_query, kv_piece = lax.optimization_barrier((w_query, kv_piece))
+    q_piece = trade(w_query, 1, 0)
+    w_out, q_piece = lax.optimization_barrier((w_out, q_piece))
     out_piece = trade(w_out, 0, 1)
     span = out_piece.shape[1]
     cut = -(-span // 256) * 128
-    w_o = [line_gather(out_piece[:, :cut], plane, planes), line_gather(out_piece[:, cut:], plane, planes)]
 
     normed = root_norm(tokens, pre_gain).astype(jnp.bfloat16)
     own = cyclic(normed, plane * span, 1)
     over_y = swap_tp(own)
     over_x = swap_seq(own, 2)
+    kv_line = hop(([kv_piece], [kv_piece]))
+    kv_line, over_y, over_x = hold(kv_line, over_y, over_x)
     half = own_rows // 2
     far = jnp.concatenate([swap_seq(over_y[:half], 2), swap_tp(over_x[half:])], axis=0)
+    for _ in range(inner_hops):
+        kv_line = hop(kv_line)
+    kv_line, far = hold(kv_line, far)
     near_rows = jnp.concatenate([own, over_y, over_x, far], axis=0)
     far_rows = swap_seq(near_rows, 1)
+
+    kv_line, q_newest = hold(kv_line, (q_piece, q_piece))
+    q_line = ([q_newest[0]], [q_newest[1]])
+    kv_line = hop(kv_line)
+    q_line = hop(q_line)
+    w_kv = jnp.concatenate(line_pieces(kv_line, plane), axis=0)
 
     flips = [(dc + 2 * dx, dy) for dc in (0, 1) for dx in (0, 1) for dy in (0, 1)]
     begins = [(seq ^ s) * block + (tp ^ t) * own_rows for s, t in flips]
     positions = jnp.concatenate([b + jnp.arange(own_rows) for b in begins])
     float_pos = positions.astype(jnp.float32)
 
-    raw_kv = jnp.concatenate(
-        [jnp.dot(r, w_kv, preferred_element_type=jnp.float32) for r in (near_rows, far_rows)], axis=0
-    )
+    raw_kv = [jnp.dot(r, w_kv, preferred_element_type=jnp.float32) for r in (near_rows, far_rows)]
+    q_line, raw_kv = hold(q_line, raw_kv)
+    for _ in range(inner_hops):
+        q_line = hop(q_line)
+    raw_kv = jnp.concatenate(raw_kv, axis=0)
     kv_width = raw_kv.shape[1] // 2
     keys = rotate_halves(raw_kv[:, :kv_width], float_pos).astype(jnp.bfloat16)
     kv_rows = jnp.concatenate([keys, raw_kv[:, kv_width:].astype(jnp.bfloat16)], axis=1)
@@ -166,12 +194,24 @@
         ordered = lax.dynamic_update_slice_in_dim(
             ordered, kv_rows[i * own_rows : (i + 1) * own_rows], b - plane * plane_rows, 0
         )
+    piece = out_piece[:, :cut]
+    q_line, ordered, piece = hold(q_line, ordered, piece)
     prior = from_behind(ordered[plane_rows - block :], "seq", PLANE)
     window = jnp.concatenate([prior, ordered], axis=0)
 
-    raw_q = jnp.concatenate(
-        [jnp.dot(r, w_q, preferred_element_type=jnp.float32) for r in (near_rows, far_rows)], axis=0
-    )
+    q_line = hop(q_line)
+    first_line = hop(([piece], [piece]))
+    w_q = jnp.concatenate(line_pieces(q_line, plane), axis=0)
+    raw_q = [jnp.dot(r, w_q, preferred_element_type=jnp.float32) for r in (near_rows, far_rows)]
+    first_line, raw_q = hold(first_line, raw_q)
+    for _ in range(inner_hops):
+        first_line = hop(first_line)
+    piece = out_piece[:, cut:]
+    first_line, piece = hold(first_line, piece)
+    first_line = hop(first_line)
+    second_line = hop(([piece], [piece]))
+    w_first = jnp.concatenate(line_pieces(first_line, plane), axis=1)
+    raw_q = jnp.concatenate(raw_q, axis=0)
     queries = (rotate_halves(raw_q, float_pos) * HEAD_SIZE ** (-0.5)).astype(jnp.bfloat16)
     firsts = [seq ^ s for s in range(PLANE)]
     firsts = [firsts[0], firsts[2], firsts[1], firsts[3]]
@@ -191,11 +231,21 @@
         block,
     ).reshape(plane_rows, -1)
 
+    def for_other_core(weights):
+        product = jnp.dot(attended[plane_rows // 2 :], weights, preferred_element_type=jnp.float32)
+        return product.astype(jnp.bfloat16)
+
+    first = for_other_core(w_first)
+    second_line, first = hold(second_line, first)
+    first = swap_seq(first, 1)
+    for _ in range(inner_hops):
+        second_line = hop(second_line)
+    second_line, first = hold(second_line, first)
+    second_line = hop(second_line)
+    w_second = jnp.concatenate(line_pieces(second_line, plane), axis=1)
+    second = swap_seq(for_other_core(w_second), 1)
     sums = []
-    for pieces in w_o:
-        weights = jnp.concatenate(pieces, axis=1)
-        theirs = jnp.dot(attended[plane_rows // 2 :], weights, preferred_element_type=jnp.float32)
-        theirs = swap_seq(theirs.astype(jnp.bfloat16), 1)
+    for weights, theirs in ((w_first, first), (w_second, second)):
         part = jnp.dot(attended[: plane_rows // 2], weights, preferred_element_type=jnp.float32)
         part = (part + theirs.astype(jnp.float32)).reshape(2, 2, own_rows, -1)
         middle = part.shape[3] // 2
@@ -243,7 +293,8 @@
 def solution(mesh):
     def body(*args):
         kv_heads = args[4].shape[1] // HEAD_SIZE
-        by_plane = kv_heads % PLANE == 0 and mesh.shape["seq"] % PLANE == 0 and mesh.shape["tp"] == 2
+        planes, rest = divmod(mesh.shape["seq"], PLANE)
+        by_plane = kv_heads % PLANE == 0 and rest == 0 and planes >= 3 and mesh.shape["tp"] == 2
         return (local_plane if by_plane else local)(*args)
 
     return jax.shard_map(

time: 477 us -> 492 us (1.031)
  blocking collectives: 0 us -> 48.6 us
  starting transfers between devices: 100 us -> 81.9 us
  matrix products: 62.2 us -> 56.7 us
    all_to_all x0 -> x1, blocking collectives: none -> 48.6 us  [trade(): lax.all_to_all(w, 'seq', split_axis=split_axis, concat_axis=concat_axis,...]
    all_to_all x3 -> x2, waiting for transfers between devices: 39.3 us -> 15.9 us  [trade(): lax.all_to_all(w, 'seq', split_axis=split_axis, concat_axis=concat_axis,...]
    ppermute x24, waiting for transfers between devices: 100 us -> 117 us  [the longest x12 69.3 us: hop(): lax.ppermute(below[-1], 'seq', up)]
    ppermute x24, starting transfers between devices: 68.8 us -> 56.2 us  [the longest x12 40 us: hop(): lax.ppermute(below[-1], 'seq', up)]
    ppermute x6, waiting for transfers between devices: 6.09 us -> 16.5 us  [swap_tp(): return lax.ppermute(x, 'tp', [(0, 1), (1, 0)])]
    concatenate x1 -> x4, other arithmetic: 2.45 us -> 9.14 us  [the longest x1 5.89 us: local_plane(): near_rows = jnp.concatenate([own, over_y, over_x, far], axis=0)]
    ppermute x9, waiting for transfers between devices: 55.7 us -> 49 us  [swap_seq(): lax.ppermute(x, 'seq', [(i, i ^ bits) for i in range(lax.axis_size('seq'))])]
    dot_general x2, matrix products: 11 us -> 6.09 us  [local_plane(): jnp.dot(attended[:plane_rows // 2], weights, preferred_element_type=jnp.f...]
  transfers between devices with their start and end apart: 43 -> 42, of which waited for: 19 -> 27; matrix products, arithmetic and copies ran while one was open for 30% -> 24% of each run, Pallas kernels for 0% -> 0%
where the time goes in v2:
time: 492 us; the launch traced here: 482 us
  waiting for transfers between devices  198 us (40%)
  starting transfers between devices  81.9 us (17%)
  matrix products  56.7 us (12%)
  other arithmetic  53 us (11%)
  blocking collectives  48.6 us (10%)
  local copies, waits for them, and re-layouts  41.8 us (8%)
    ppermute x12, waiting for transfers between devices, hop(): lax.ppermute(below[-1], 'seq', up)  69.3 us
    ppermute x9, waiting for transfers between devices, swap_seq(): lax.ppermute(x, 'seq', [(i, i ^ bits) for i in range(lax.axis_size('seq'))])  49 us
    all_to_all x1, blocking collectives, trade(): lax.all_to_all(w, 'seq', split_axis=split_axis, concat_axis=concat_axis,...  48.6 us
    ppermute x12, waiting for transfers between devices, hop(): lax.ppermute(above[-1], 'seq', down)  47.4 us
    ppermute x12, starting transfers between devices, hop(): lax.ppermute(below[-1], 'seq', up)  40 us
    ppermute x6, waiting for transfers between devices, swap_tp(): return lax.ppermute(x, 'tp', [(0, 1), (1, 0)])  16.5 us
    ppermute x12, starting transfers between devices, hop(): lax.ppermute(above[-1], 'seq', down)  16.2 us
    all_to_all x2, waiting for transfers between devices, trade(): lax.all_to_all(w, 'seq', split_axis=split_axis, concat_axis=concat_axis,...  15.9 us
  transfers between devices with their start and end apart: 42, of which 27 were waited for; matrix products, arithmetic and copies ran while one was open for 24% of the time, Pallas kernels for 0%

profile of v2, /device:TPU:0, one launch (start us, length us, event | category | flops | bytes accessed | tf_op | source)
XLA Modules:
  0.0 482.0 jit_solution(3867254794978468902)
XLA Ops:
  10.6 48.6 %all_to_all.54 = bf16[224,4,512]{2,0,1:T(8,128)(2,1)S(1)} all-to-all(bf16[224,4,512]{2,0,1:T(8,128)(2,1)S(1)} %copy.33), channel_id=1, replica_groups={{0,2,4,6},{8,10,12,14},{16,18,20,22},{24,26,28,30},{1,3,5,7},{9,11,13,1..., dimensions={1} | all-to-all | bytes 1835008 | tf_op jit(solution)/shard_map/all_to_all | solution.py:139
  64.0 17.9 %collective-permute-done = bf16[896,512]{1,0:T(8,128)(2,1)S(1)} collective-permute-done((bf16[896,512]{1,0:T(8,128)(2,1)S(1)}, bf16[896,512]{1,0:T(8,128)(2,1)S(1)}, u32[]{:S(2)}, u32[]{:S(2)}) %collective-permute-start) | collective-permute-done | bytes 917536 | tf_op jit(solution)/shard_map/ppermute | solution.py:79
  95.8 12.5 %collective-permute-done.6 = bf16[128,3584]{1,0:T(8,128)(2,1)S(1)} collective-permute-done((bf16[128,3584]{1,0:T(8,128)(2,1)S(1)}, bf16[128,3584]{1,0:T(8,128)(2,1)S(1)}, u32[]{:S(2)}, u32[]{:S(2)}) %collective-permute-start.6) | collective-permute-done | bytes 917536 | tf_op jit(solution)/shard_map/ppermute | solution.py:17
  116.1 5.9 %pad_maximum_fusion = bf16[1024,3584]{1,0:T(8,128)(2,1)} fusion(bf16[256,3584]{1,0:T(8,128)(2,1)S(1)} %pad_maximum_fusion.8, bf16[256,3584]{1,0:T(8,128)(2,1)} %collective-permute-done.3, bf16[256,3584]{1,0:T(8,128)(2,1)} %collective-permute-done.2, bf16[256,3584]{1,0:T(8,128)(2,1)S(1)} %copy-done.6), kind=kLoop, calls=%fused_computation.11 | loop fusion | flops 29360128 | bytes 14680064 | tf_op jit(solution)/shard_map/concatenate | solution.py:169
  126.9 12.8 %all-to-all-done.1 = bf16[224,4,512]{2,0,1:T(8,128)(2,1)S(1)} async-done(((bf16[224,4,512]{2,0,1:T(8,128)(2,1)}), bf16[224,4,512]{2,0,1:T(8,128)(2,1)S(1)}, u32[]{:S(2)}, u32[]{:S(2)}) %all-to-all-start.1) | async-done | bytes 917536 | tf_op jit(solution)/shard_map/all_to_all | solution.py:139
  170.4 5.2 %collective-permute-done.11 = bf16[896,512]{1,0:T(8,128)(2,1)} collective-permute-done((bf16[896,512]{1,0:T(8,128)(2,1)}, bf16[896,512]{1,0:T(8,128)(2,1)}, u32[]{:S(2)}, u32[]{:S(2)}) %collective-permute-start.11) | collective-permute-done | bytes 917536 | tf_op jit(solution)/shard_map/ppermute | solution.py:80
  176.9 6.0 %fusion.43 = f32[1024,512]{1,0:T(8,128)S(1)} fusion(bf16[896,512]{1,0:T(8,128)(2,1)S(1)} %broadcast_select_fusion.1, bf16[896,512]{1,0:T(8,128)(2,1)S(1)} %broadcast_select_fusion.3, bf16[896,512]{1,0:T(8,128)(2,1)S(1)} %broadcast_select_fusion.5, bf16[896,512]{1,0:T(8,128)(2,1)S(1)} %bitcast.155, bf16[256,3584]{1,0:T(8,128)(2,1)S(1)} %pad_maximum_fusion.8, ...), kind=kOutput, calls=%fused_computation.124 | convolution fusion | flops 3802136576 | bytes 13107200 | tf_op jit(solution)/shard_map/dot_general | solution.py:183
  182.9 7.0 %fusion.42 = f32[1024,512]{1,0:T(8,128)S(1)} fusion(bf16[1024,3584]{1,0:T(8,128)(2,1)} %collective-permute-done.12, bf16[896,512]{1,0:T(8,128)(2,1)S(1)} %broadcast_select_fusion.1, bf16[896,512]{1,0:T(8,128)(2,1)S(1)} %broadcast_select_fusion.3, bf16[896,512]{1,0:T(8,128)(2,1)S(1)} %broadcast_select_fusion.5, bf16[896,512]{1,0:T(8,128)(2,1)S(1)} %bitcast.156), kind=kOutput, calls=%fused_computation.123 | convolution fusion | flops 3772776448 | bytes 13107200 | tf_op jit(solution)/shard_map/dot_general | solution.py:183
  203.4 12.3 %collective-permute-done.13 = bf16[896,512]{1,0:T(8,128)(2,1)S(1)} collective-permute-done((bf16[896,512]{1,0:T(8,128)(2,1)S(1)}, bf16[896,512]{1,0:T(8,128)(2,1)S(1)}, u32[]{:S(2)}, u32[]{:S(2)}) %collective-permute-start.13) | collective-permute-done | bytes 917536 | tf_op jit(solution)/shard_map/ppermute | solution.py:79
  224.0 5.4 %multiply_cosine_fusion = (f32[2048,128]{1,0:T(8,128)S(1)}, f32[2048,128]{1,0:T(8,128)}) fusion(f32[128]{0:T(128)S(1)} %negate_power_fusion, f32[2048]{0:T(1024)S(1)} %convert_element_type.115), kind=kLoop, calls=%fused_computation.80 | loop fusion | flops 262144 | bytes 2105856 | tf_op jit(solution)/shard_map/cos | solution.py:35
  245.0 19.2 %collective-permute-done.18 = bf16[896,512]{1,0:T(8,128)(2,1)S(1)} collective-permute-done((bf16[896,512]{1,0:T(8,128)(2,1)}, bf16[896,512]{1,0:T(8,128)(2,1)S(1)}, u32[]{:S(2)}, u32[]{:S(2)}) %collective-permute-start.18) | collective-permute-done | bytes 917536 | tf_op jit(solution)/shard_map/ppermute | solution.py:79
  266.6 6.0 %fusion.41 = f32[1024,512]{1,0:T(8,128)S(1)} fusion(bf16[896,512]{1,0:T(8,128)(2,1)S(1)} %broadcast_select_fusion, bf16[896,512]{1,0:T(8,128)(2,1)S(1)} %broadcast_select_fusion.2, bf16[896,512]{1,0:T(8,128)(2,1)S(1)} %broadcast_select_fusion.4, bf16[896,512]{1,0:T(8,128)(2,1)S(1)} %bitcast.151, bf16[256,3584]{1,0:T(8,128)(2,1)S(1)} %copy-done.4, ...), kind=kOutput, calls=%fused_computation.122 | convolution fusion | flops 3802136576 | bytes 13107200 | tf_op jit(solution)/shard_map/dot_general | solution.py:205
  272.6 7.0 %fusion.40 = f32[1024,512]{1,0:T(8,128)S(1)} fusion(bf16[1024,3584]{1,0:T(8,128)(2,1)} %collective-permute-done.12, bf16[896,512]{1,0:T(8,128)(2,1)S(1)} %broadcast_select_fusion, bf16[896,512]{1,0:T(8,128)(2,1)S(1)} %broadcast_select_fusion.2, bf16[896,512]{1,0:T(8,128)(2,1)S(1)} %broadcast_select_fusion.4, bf16[896,512]{1,0:T(8,128)(2,1)S(1)} %bitcast.152), kind=kOutput, calls=%fused_computation.121 | convolution fusion | flops 3772776448 | bytes 13107200 | tf_op jit(solution)/shard_map/dot_general | solution.py:205
  286.6 5.9 %reshape.289 = f32[2048,2,256]{2,1,0:T(2,128)} reshape(f32[2048,512]{1,0:T(8,128)} %pad_maximum_fusion.2) | data formatting | bytes 8388608 | tf_op jit(solution)/shard_map/reshape | solution.py:31
  298.3 7.9 %fusion = (f32[4,2,512]{2,1,0:T(2,128)S(1)}, f32[4,1024,512,2]{2,1,3,0:T(8,128)}) fusion(pred[4,512,1024]{1,2,0:T(8,128)(4,1)S(1)} %copy-done.15, bf16[4,512,2,256]{3,1,0,2:T(8,128)(2,1)S(1)} %bitcast.142, bf16[4,1024,512]{2,1,0:T(8,128)(2,1)S(1)} %copy-done.13), kind=kOutput, calls=%fused_computation.1 | convolution fusion | flops 2155868160 | bytes 23085056 | tf_op jit(solution)/shard_map/bqhd,bkd->bhqk/dot_general | solution.py:105
  306.2 10.8 %fusion.9 = bf16[4,512,2,256]{1,3,2,0:T(8,128)(2,1)} fusion(f32[4,1024,512,2]{2,1,3,0:T(8,128)} %get-tuple-element.94, pred[4,512,1024]{1,2,0:T(8,128)(4,1)S(1)} %copy-done.15, bf16[4,1024,512]{2,1,0:T(8,128)(2,1)S(1)} %copy-done.13, f32[4,512,2]{1,2,0:T(2,128)S(1)} %bitcast.157), kind=kOutput, calls=%fused_computation.24 | convolution fusion | flops 2157969408 | bytes 23085056 | tf_op jit(solution)/shard_map/bhqk,bkd->bqhd/dot_general | solution.py:110
  317.1 5.3 %collective-permute-start.22 = (bf16[512,512]{0,1:T(8,128)(2,1)}, bf16[512,512]{0,1:T(8,128)(2,1)}, u32[]{:S(2)}, u32[]{:S(2)}) collective-permute-start(bf16[512,512]{0,1:T(8,128)(2,1)} %collective-permute-done.20), channel_id=1, source_target_pairs={{0,8},{2,10},{4,12},{6,14},{8,16},{10,18},{12,20},{14,22},{16,24},... | collective-permute-start | bytes 1572872 | tf_op jit(solution)/shard_map/ppermute | solution.py:79
  335.4 12.2 %collective-permute-done.23 = bf16[512,512]{0,1:T(8,128)(2,1)S(1)} collective-permute-done((bf16[512,512]{0,1:T(8,128)(2,1)}, bf16[512,512]{0,1:T(8,128)(2,1)S(1)}, u32[]{:S(2)}, u32[]{:S(2)}) %collective-permute-start.23) | collective-permute-done | bytes 524320 | tf_op jit(solution)/shard_map/ppermute | solution.py:80
  356.1 7.0 %collective-permute-done.26 = bf16[512,384]{0,1:T(8,128)(2,1)} collective-permute-done((bf16[512,384]{0,1:T(8,128)(2,1)S(1)}, bf16[512,384]{0,1:T(8,128)(2,1)}, u32[]{:S(2)}, u32[]{:S(2)}) %collective-permute-start.26) | collective-permute-done | bytes 393248 | tf_op jit(solution)/shard_map/ppermute | solution.py:79
  363.1 4.9 %collective-permute-done.27 = bf16[512,384]{0,1:T(8,128)(2,1)S(1)} collective-permute-done((bf16[512,384]{0,1:T(8,128)(2,1)S(1)}, bf16[512,384]{0,1:T(8,128)(2,1)S(1)}, u32[]{:S(2)}, u32[]{:S(2)}) %collective-permute-start.27) | collective-permute-done | bytes 393248 | tf_op jit(solution)/shard_map/ppermute | solution.py:80
  377.8 6.2 %collective-permute-done.34 = bf16[512,384]{0,1:T(8,128)(2,1)S(1)} collective-permute-done((bf16[512,384]{0,1:T(8,128)(2,1)}, bf16[512,384]{0,1:T(8,128)(2,1)S(1)}, u32[]{:S(2)}, u32[]{:S(2)}) %collective-permute-start.34) | collective-permute-done | bytes 393248 | tf_op jit(solution)/shard_map/ppermute | solution.py:80
  398.4 18.7 %collective-permute-done.29 = bf16[2,256,1024]{2,1,0:T(8,128)(2,1)S(1)} collective-permute-done((bf16[2,256,1024]{2,1,0:T(8,128)(2,1)}, bf16[2,256,1024]{2,1,0:T(8,128)(2,1)S(1)}, u32[]{:S(2)}, u32[]{:S(2)}) %collective-permute-start.29) | collective-permute-done | bytes 1048608 | tf_op jit(solution)/shard_map/ppermute | solution.py:17
  424.3 9.6 %collective-permute-done.30 = bf16[256,1024]{1,0:T(8,128)(2,1)S(1)} collective-permute-done((bf16[256,1024]{1,0:T(8,128)(2,1)S(1)}, bf16[256,1024]{1,0:T(8,128)(2,1)S(1)}, u32[]{:S(2)}, u32[]{:S(2)}) %collective-permute-start.30) | collective-permute-done | bytes 524320 | tf_op jit(solution)/shard_map/ppermute | solution.py:21
  440.7 16.4 %collective-permute-done.36 = bf16[2,256,768]{2,1,0:T(8,128)(2,1)S(1)} collective-permute-done((bf16[2,256,768]{2,1,0:T(8,128)(2,1)S(1)}, bf16[2,256,768]{2,1,0:T(8,128)(2,1)S(1)}, u32[]{:S(2)}, u32[]{:S(2)}) %collective-permute-start.36) | collective-permute-done | bytes 786464 | tf_op jit(solution)/shard_map/ppermute | solution.py:17
  (291 shorter events, 209.5 us)
Async XLA Ops:
  4.8 81.2 %collective-permute-start.2 = (bf16[256,3584]{1,0:T(8,128)(2,1)S(1)}, bf16[256,3584]{1,0:T(8,128)(2,1)}, u32[]{:S(2)}, u32[]{:S(2)}) collective-permute-start(bf16[256,3584]{1,0:T(8,128)(2,1)S(1)} %fusion.21), channel_id=1, source_target_pairs={{0,1},{1,0},{2,3},{3,2},{4,5},{5,4},{6,7},{7,6},{8,9},{9,8},{10,11... | collective-permute-start | bytes 5505032 | tf_op jit(solution)/shard_map/ppermute | solution.py:21
  7.8 78.2 %collective-permute-start.3 = (bf16[256,3584]{1,0:T(8,128)(2,1)S(1)}, bf16[256,3584]{1,0:T(8,128)(2,1)}, u32[]{:S(2)}, u32[]{:S(2)}) collective-permute-start(bf16[256,3584]{1,0:T(8,128)(2,1)S(1)} %fusion.21), channel_id=1, source_target_pairs={{0,4},{2,6},{4,0},{6,2},{8,12},{10,14},{12,8},{14,10},{16,20},{18,... | collective-permute-start | bytes 5505032 | tf_op jit(solution)/shard_map/ppermute | solution.py:17
  59.1 22.7 %collective-permute-start = (bf16[896,512]{1,0:T(8,128)(2,1)S(1)}, bf16[896,512]{1,0:T(8,128)(2,1)S(1)}, u32[]{:S(2)}, u32[]{:S(2)}) collective-permute-start(bf16[896,512]{1,0:T(8,128)(2,1)S(1)} %bitcast.153), channel_id=1, source_target_pairs={{0,8},{2,10},{4,12},{6,14},{8,16},{10,18},{12,20},{14,22},{16,24},... | collective-permute-start | bytes 2752520 | tf_op jit(solution)/shard_map/ppermute | solution.py:79
  62.7 23.3 %collective-permute-start.1 = (bf16[896,512]{1,0:T(8,128)(2,1)S(1)}, bf16[896,512]{1,0:T(8,128)(2,1)S(1)}, u32[]{:S(2)}, u32[]{:S(2)}) collective-permute-start(bf16[896,512]{1,0:T(8,128)(2,1)S(1)} %bitcast.154), channel_id=1, source_target_pairs={{8,0},{10,2},{12,4},{14,6},{16,8},{18,10},{20,12},{22,14},{24,16},... | collective-permute-start | bytes 2752520 | tf_op jit(solution)/shard_map/ppermute | solution.py:80
  87.6 20.7 %collective-permute-start.6 = (bf16[128,3584]{1,0:T(8,128)(2,1)S(1)}, bf16[128,3584]{1,0:T(8,128)(2,1)S(1)}, u32[]{:S(2)}, u32[]{:S(2)}) collective-permute-start(bf16[128,3584]{1,0:T(8,128)(2,1)S(1)} %slice.146), channel_id=1, source_target_pairs={{0,4},{2,6},{4,0},{6,2},{8,12},{10,14},{12,8},{14,10},{16,20},{18,... | collective-permute-start | bytes 2752520 | tf_op jit(solution)/shard_map/ppermute | solution.py:17
  91.0 21.0 %collective-permute-start.4 = (bf16[896,512]{1,0:T(8,128)(2,1)S(1)}, bf16[896,512]{1,0:T(8,128)(2,1)S(1)}, u32[]{:S(2)}, u32[]{:S(2)}) collective-permute-start(bf16[896,512]{1,0:T(8,128)(2,1)S(1)} %collective-permute-done), channel_id=1, source_target_pairs={{0,8},{2,10},{4,12},{6,14},{8,16},{10,18},{12,20},{14,22},{16,24},... | collective-permute-start | bytes 2752520 | tf_op jit(solution)/shard_map/ppermute | solution.py:79
  94.5 21.6 %collective-permute-start.5 = (bf16[896,512]{1,0:T(8,128)(2,1)S(1)}, bf16[896,512]{1,0:T(8,128)(2,1)S(1)}, u32[]{:S(2)}, u32[]{:S(2)}) collective-permute-start(bf16[896,512]{1,0:T(8,128)(2,1)S(1)} %collective-permute-done.1), channel_id=1, source_target_pairs={{8,0},{10,2},{12,4},{14,6},{16,8},{18,10},{20,12},{22,14},{24,16},... | collective-permute-start | bytes 2752520 | tf_op jit(solution)/shard_map/ppermute | solution.py:80
  122.0 60.9 %collective-permute-start.12 = (bf16[1024,3584]{1,0:T(8,128)(2,1)}, bf16[1024,3584]{1,0:T(8,128)(2,1)}, u32[]{:S(2)}, u32[]{:S(2)}) collective-permute-start(bf16[1024,3584]{1,0:T(8,128)(2,1)} %pad_maximum_fusion), channel_id=1, source_target_pairs={{0,2},{2,0},{4,6},{6,4},{8,10},{10,8},{12,14},{14,12},{16,18},{18,... | collective-permute-start | bytes 22020104 | tf_op jit(solution)/shard_map/ppermute | solution.py:17
  145.7 24.5 %collective-permute-start.10 = (bf16[896,512]{1,0:T(8,128)(2,1)}, bf16[896,512]{1,0:T(8,128)(2,1)}, u32[]{:S(2)}, u32[]{:S(2)}) collective-permute-start(bf16[896,512]{1,0:T(8,128)(2,1)} %copy-done.28), channel_id=1, source_target_pairs={{0,8},{2,10},{4,12},{6,14},{8,16},{10,18},{12,20},{14,22},{16,24},... | collective-permute-start | bytes 2752520 | tf_op jit(solution)/shard_map/ppermute | solution.py:79
  150.1 25.4 %collective-permute-start.11 = (bf16[896,512]{1,0:T(8,128)(2,1)}, bf16[896,512]{1,0:T(8,128)(2,1)}, u32[]{:S(2)}, u32[]{:S(2)}) collective-permute-start(bf16[896,512]{1,0:T(8,128)(2,1)} %copy-done.27), channel_id=1, source_target_pairs={{8,0},{10,2},{12,4},{14,6},{16,8},{18,10},{20,12},{22,14},{24,16},... | collective-permute-start | bytes 2752520 | tf_op jit(solution)/shard_map/ppermute | solution.py:80
  159.6 30.3 %collective-permute-start.8 = (bf16[896,512]{1,0:T(8,128)(2,1)}, bf16[896,512]{1,0:T(8,128)(2,1)S(1)}, u32[]{:S(2)}, u32[]{:S(2)}) collective-permute-start(bf16[896,512]{1,0:T(8,128)(2,1)} %bitcast.149), channel_id=1, source_target_pairs={{0,8},{2,10},{4,12},{6,14},{8,16},{10,18},{12,20},{14,22},{16,24},... | collective-permute-start | bytes 2752520 | tf_op jit(solution)/shard_map/ppermute | solution.py:79
  163.2 31.1 %collective-permute-start.9 = (bf16[896,512]{1,0:T(8,128)(2,1)}, bf16[896,512]{1,0:T(8,128)(2,1)S(1)}, u32[]{:S(2)}, u32[]{:S(2)}) collective-permute-start(bf16[896,512]{1,0:T(8,128)(2,1)} %bitcast.150), channel_id=1, source_target_pairs={{8,0},{10,2},{12,4},{14,6},{16,8},{18,10},{20,12},{22,14},{24,16},... | collective-permute-start | bytes 2752520 | tf_op jit(solution)/shard_map/ppermute | solution.py:80
  196.7 23.2 %collective-permute-start.14 = (bf16[896,512]{1,0:T(8,128)(2,1)S(1)}, bf16[896,512]{1,0:T(8,128)(2,1)S(1)}, u32[]{:S(2)}, u32[]{:S(2)}) collective-permute-start(bf16[896,512]{1,0:T(8,128)(2,1)S(1)} %collective-permute-done.9), channel_id=1, source_target_pairs={{8,0},{10,2},{12,4},{14,6},{16,8},{18,10},{20,12},{22,14},{24,16},... | collective-permute-start | bytes 2752520 | tf_op jit(solution)/shard_map/ppermute | solution.py:80
  230.4 49.2 %collective-permute-start.16 = (bf16[512,512]{0,1:T(8,128)(2,1)}, bf16[512,512]{0,1:T(8,128)(2,1)}, u32[]{:S(2)}, u32[]{:S(2)}) collective-permute-start(bf16[512,512]{0,1:T(8,128)(2,1)} %slice.207), channel_id=1, source_target_pairs={{0,8},{2,10},{4,12},{6,14},{8,16},{10,18},{12,20},{14,22},{16,24},... | collective-permute-start | bytes 1572872 | tf_op jit(solution)/shard_map/ppermute | solution.py:79
  232.7 46.9 %collective-permute-start.17 = (bf16[512,512]{0,1:T(8,128)(2,1)}, bf16[512,512]{0,1:T(8,128)(2,1)}, u32[]{:S(2)}, u32[]{:S(2)}) collective-permute-start(bf16[512,512]{0,1:T(8,128)(2,1)} %slice.207), channel_id=1, source_target_pairs={{8,0},{10,2},{12,4},{14,6},{16,8},{18,10},{20,12},{22,14},{24,16},... | collective-permute-start | bytes 1572872 | tf_op jit(solution)/shard_map/ppermute | solution.py:80
  234.0 30.3 %collective-permute-start.18 = (bf16[896,512]{1,0:T(8,128)(2,1)}, bf16[896,512]{1,0:T(8,128)(2,1)S(1)}, u32[]{:S(2)}, u32[]{:S(2)}) collective-permute-start(bf16[896,512]{1,0:T(8,128)(2,1)} %copy-done.34), channel_id=1, source_target_pairs={{0,8},{2,10},{4,12},{6,14},{8,16},{10,18},{12,20},{14,22},{16,24},... | collective-permute-start | bytes 2752520 | tf_op jit(solution)/shard_map/ppermute | solution.py:79
  238.6 27.9 %collective-permute-start.19 = (bf16[896,512]{1,0:T(8,128)(2,1)}, bf16[896,512]{1,0:T(8,128)(2,1)S(1)}, u32[]{:S(2)}, u32[]{:S(2)}) collective-permute-start(bf16[896,512]{1,0:T(8,128)(2,1)} %copy-done.33), channel_id=1, source_target_pairs={{8,0},{10,2},{12,4},{14,6},{16,8},{18,10},{20,12},{22,14},{24,16},... | collective-permute-start | bytes 2752520 | tf_op jit(solution)/shard_map/ppermute | solution.py:80
  279.6 37.5 %collective-permute-start.20 = (bf16[512,512]{0,1:T(8,128)(2,1)}, bf16[512,512]{0,1:T(8,128)(2,1)}, u32[]{:S(2)}, u32[]{:S(2)}) collective-permute-start(bf16[512,512]{0,1:T(8,128)(2,1)} %collective-permute-done.16), channel_id=1, source_target_pairs={{0,8},{2,10},{4,12},{6,14},{8,16},{10,18},{12,20},{14,22},{16,24},... | collective-permute-start | bytes 1572872 | tf_op jit(solution)/shard_map/ppermute | solution.py:79
  282.6 34.5 %collective-permute-start.21 = (bf16[512,512]{0,1:T(8,128)(2,1)}, bf16[512,512]{0,1:T(8,128)(2,1)}, u32[]{:S(2)}, u32[]{:S(2)}) collective-permute-start(bf16[512,512]{0,1:T(8,128)(2,1)} %collective-permute-done.17), channel_id=1, source_target_pairs={{8,0},{10,2},{12,4},{14,6},{16,8},{18,10},{20,12},{22,14},{24,16},... | collective-permute-start | bytes 1572872 | tf_op jit(solution)/shard_map/ppermute | solution.py:80
  325.3 24.7 %collective-permute-start.24 = (bf16[512,384]{0,1:T(8,128)(2,1)S(1)}, bf16[512,384]{0,1:T(8,128)(2,1)S(1)}, u32[]{:S(2)}, u32[]{:S(2)}) collective-permute-start(bf16[512,384]{0,1:T(8,128)(2,1)S(1)} %slice.213), channel_id=1, source_target_pairs={{0,8},{2,10},{4,12},{6,14},{8,16},{10,18},{12,20},{14,22},{16,24},... | collective-permute-start | bytes 1179656 | tf_op jit(solution)/shard_map/ppermute | solution.py:79
  326.7 23.4 %collective-permute-start.25 = (bf16[512,384]{0,1:T(8,128)(2,1)S(1)}, bf16[512,384]{0,1:T(8,128)(2,1)S(1)}, u32[]{:S(2)}, u32[]{:S(2)}) collective-permute-start(bf16[512,384]{0,1:T(8,128)(2,1)S(1)} %slice.213), channel_id=1, source_target_pairs={{8,0},{10,2},{12,4},{14,6},{16,8},{18,10},{20,12},{22,14},{24,16},... | collective-permute-start | bytes 1179656 | tf_op jit(solution)/shard_map/ppermute | solution.py:80
  387.5 46.5 %collective-permute-start.35 = (bf16[1024,1536]{1,0:T(8,128)(2,1)}, bf16[1024,1536]{1,0:T(8,128)(2,1)}, u32[]{:S(2)}, u32[]{:S(2)}) collective-permute-start(bf16[1024,1536]{1,0:T(8,128)(2,1)} %convolution_convert_fusion), channel_id=1, source_target_pairs={{0,2},{2,0},{4,6},{6,4},{8,10},{10,8},{12,14},{14,12},{16,18},{18,... | collective-permute-start | bytes 9437192 | tf_op jit(solution)/shard_map/ppermute | solution.py:17
  391.4 25.7 %collective-permute-start.29 = (bf16[2,256,1024]{2,1,0:T(8,128)(2,1)}, bf16[2,256,1024]{2,1,0:T(8,128)(2,1)S(1)}, u32[]{:S(2)}, u32[]{:S(2)}) collective-permute-start(bf16[2,256,1024]{2,1,0:T(8,128)(2,1)} %fusion.32), channel_id=1, source_target_pairs={{0,4},{2,6},{4,0},{6,2},{8,12},{10,14},{12,8},{14,10},{16,20},{18,... | collective-permute-start | bytes 3145736 | tf_op jit(solution)/shard_map/ppermute | solution.py:17
  396.9 26.2 %collective-permute-start.31 = (bf16[2,256,1024]{2,1,0:T(8,128)(2,1)}, bf16[2,256,1024]{2,1,0:T(8,128)(2,1)S(1)}, u32[]{:S(2)}, u32[]{:S(2)}) collective-permute-start(bf16[2,256,1024]{2,1,0:T(8,128)(2,1)} %fusion.33), channel_id=1, source_target_pairs={{0,1},{1,0},{2,3},{3,2},{4,5},{5,4},{6,7},{7,6},{8,9},{9,8},{10,11... | collective-permute-start | bytes 3145736 | tf_op jit(solution)/shard_map/ppermute | solution.py:21
  (77 other events, 1045.2 us)

commit v3 on v0

--- a/solution.py
+++ b/solution.py
@@ -64,7 +64,17 @@
 
 def local(tokens, pre_gain, post_gain, w_query, key_matrix, value_matrix, w_out):
     normalized_input = root_norm(tokens, pre_gain).astype(jnp.bfloat16)
-    gathered = lax.all_gather(normalized_input, "tp", axis=0, tiled=True)
+    tp = lax.axis_index("tp")
+    two = lax.axis_size("tp") == 2
+    if two:
+        peer = lax.ppermute(normalized_input, "tp", [(0, 1), (1, 0)])
+        gathered = jnp.where(
+            tp == 0,
+            jnp.concatenate([normalized_input, peer], axis=0),
+            jnp.concatenate([peer, normalized_input], axis=0),
+        )
+    else:
+        gathered = lax.all_gather(normalized_input, "tp", axis=0, tiled=True)
     pieces = (
         lax.all_gather(w_query, "seq", axis=0, tiled=True),
         lax.all_gather(key_matrix, "seq", axis=0, tiled=True),
@@ -85,9 +95,16 @@
         lax.all_gather(w_out, "seq", axis=1, tiled=True),
         preferred_element_type=jnp.float32,
     )
-    own_rows = lax.psum_scatter(
-        partial_value.astype(jnp.bfloat16), "tp", scatter_dimension=0, tiled=True
-    ).astype(jnp.float32)
+    if two:
+        count = tokens.shape[0]
+        kept = lax.dynamic_slice_in_dim(partial_value, tp * count, count, 0)
+        sent = lax.dynamic_slice_in_dim(partial_value, (1 - tp) * count, count, 0)
+        came = lax.ppermute(sent.astype(jnp.bfloat16), "tp", [(0, 1), (1, 0)])
+        own_rows = kept.astype(jnp.bfloat16).astype(jnp.float32) + came.astype(jnp.float32)
+    else:
+        own_rows = lax.psum_scatter(
+            partial_value.astype(jnp.bfloat16), "tp", scatter_dimension=0, tiled=True
+        ).astype(jnp.float32)
     mixed = root_norm(own_rows, post_gain)
     return (tokens.astype(jnp.float32) + mixed).astype(jnp.bfloat16)
 

time: 519 us -> 458 us (0.88)
  waiting for transfers between devices: 411 us -> 331 us
  local copies, waits for them, and re-layouts: 8.96 us -> 15.6 us
  matrix products: 60 us -> 66.4 us
    ppermute x0 -> x2, waiting for transfers between devices: none -> 80.3 us  [the longest x1 41 us: local(): came = lax.ppermute(sent.astype(jnp.bfloat16), 'tp', [(0, 1), (1, 0)])]
    all_gather x1 -> x0, waiting for transfers between devices: 50 us -> none  [local(): gathered = lax.all_gather(normalized_input, 'tp', axis=0, tiled=True)]
    reduce_scatter x1 -> x0, waiting for transfers between devices: 47.5 us -> none  [local(): lax.psum_scatter(partial_value.astype(jnp.bfloat16), 'tp', scatter_dimens...]
    all_gather x1, waiting for transfers between devices: 70 us -> 25.2 us  [local(): lax.all_gather(value_matrix, 'seq', axis=0, tiled=True)]
    all_gather x1, waiting for transfers between devices: 99.3 us -> 88.8 us  [local(): lax.all_gather(w_query, 'seq', axis=0, tiled=True)]
    dot_general x3, matrix products: 30.7 us -> 36.3 us  [local(): jnp.dot(gathered, piece, preferred_element_type=jnp.float32)]
    all_gather x1, waiting for transfers between devices: 80.6 us -> 75.4 us  [local(): lax.all_gather(w_out, 'seq', axis=1, tiled=True)]
  transfers between devices with their start and end apart: 8 -> 8, of which waited for: 6 -> 6; matrix products, arithmetic and copies ran while one was open for 12% -> 17% of each run, Pallas kernels for 0% -> 0%
where the time goes in v3:
time: 458 us
  waiting for transfers between devices  331 us (72%)
  matrix products  66.4 us (14%)
  other arithmetic  20.5 us (4%)
  local copies, waits for them, and re-layouts  15.6 us (3%)
  between operations  13.3 us (3%)
  starting transfers between devices  10.9 us (2%)
    all_gather x1, waiting for transfers between devices, local(): lax.all_gather(w_query, 'seq', axis=0, tiled=True)  88.8 us
    all_gather x1, waiting for transfers between devices, local(): lax.all_gather(w_out, 'seq', axis=1, tiled=True)  75.4 us
    all_gather x1, waiting for transfers between devices, local(): lax.all_gather(key_matrix, 'seq', axis=0, tiled=True)  59 us
    ppermute x1, waiting for transfers between devices, local(): came = lax.ppermute(sent.astype(jnp.bfloat16), 'tp', [(0, 1), (1, 0)])  41 us
    ppermute x1, waiting for transfers between devices, local(): peer = lax.ppermute(normalized_input, 'tp', [(0, 1), (1, 0)])  39.3 us
    dot_general x3, matrix products, local(): jnp.dot(gathered, piece, preferred_element_type=jnp.float32)  36.3 us
    all_gather x1, waiting for transfers between devices, local(): lax.all_gather(value_matrix, 'seq', axis=0, tiled=True)  25.2 us
    dot_general x1, matrix products, local(): jnp.dot(attended, lax.all_gather(w_out, 'seq', axis=1, tiled=True), prefe...  11.7 us
  transfers between devices with their start and end apart: 8, of which 6 were waited for; matrix products, arithmetic and copies ran while one was open for 17% of the time, Pallas kernels for 0%

profile of v3, /device:TPU:0, one launch (start us, length us, event | category | flops | bytes accessed | tf_op | source)
XLA Modules:
  0.0 458.0 jit_solution(15770798965883437257)
XLA Ops:
  11.5 3.0 collective-permute-start
  15.5 39.3 %collective-permute-done = bf16[256,3584]{1,0:T(8,128)(2,1)} collective-permute-done((bf16[256,3584]{1,0:T(8,128)(2,1)}, bf16[256,3584]{1,0:T(8,128)(2,1)}, u32[]{:S(2)}, u32[]{:S(2)}) %collective-permute-start) | collective-permute-done | bytes 1835040 | tf_op jit(solution)/shard_map/ppermute | solution.py:70
  54.9 25.2 %all-gather.5.cloned.1.call-done = bf16[3584,1024]{1,0:T(8,128)(2,1)} async-done(((bf16[224,1024]{1,0:T(8,128)(2,1)}), bf16[3584,1024]{1,0:T(8,128)(2,1)}) %all-gather.5.cloned.1.call-update) | async-done | bytes 7340048 | tf_op jit(solution)/shard_map/all_gather | solution.py:81
  80.0 10.3 %convolution_convert_fusion = bf16[512,1024]{1,0:T(8,128)(2,1)} fusion(bf16[3584,1024]{1,0:T(8,128)(2,1)} %all-gather.5.cloned.1.call-done, bf16[256,3584]{1,0:T(8,128)(2,1)} %collective-permute-done, bf16[256,3584]{1,0:T(8,128)(2,1)} %fusion.10, pred[]{:T(512)S(6)} %eq.3), kind=kOutput, calls=%fused_computation.30 | convolution fusion | flops 3775135744 | bytes 12058625 | tf_op jit(solution)/shard_map/dot_general | solution.py:84
  90.4 3.2 collective-permute-start.1
  93.5 59.0 %all-gather.7.cloned.1.call-done = bf16[3584,1024]{1,0:T(8,128)(2,1)} async-done(((bf16[224,1024]{1,0:T(8,128)(2,1)}), bf16[3584,1024]{1,0:T(8,128)(2,1)}) %all-gather.7.cloned.1.call-update) | async-done | bytes 7340048 | tf_op jit(solution)/shard_map/all_gather | solution.py:80
  152.5 10.7 %fusion.18 = f32[512,1024]{1,0:T(8,128)} fusion(bf16[3584,1024]{1,0:T(8,128)(2,1)} %all-gather.7.cloned.1.call-done, bf16[256,3584]{1,0:T(8,128)(2,1)} %collective-permute-done, bf16[256,3584]{1,0:T(8,128)(2,1)} %fusion.10, pred[]{:T(512)S(6)} %eq.3), kind=kOutput, calls=%fused_computation.44 | convolution fusion | flops 3774611456 | bytes 13107201 | tf_op jit(solution)/shard_map/dot_general | solution.py:84
  163.2 3.2 reshape.114
  166.4 2.1 subtract_convert_fusion
  170.8 3.1 collective-permute-start.2
  175.2 3.1 pad_maximum_fusion
  178.3 3.9 copy.19
  182.3 2.9 pad_maximum_fusion.1
  185.2 88.8 %all-gather.9.cloned.1.call-done = bf16[3584,2048]{1,0:T(8,128)(2,1)} async-done(((bf16[224,2048]{1,0:T(8,128)(2,1)}), bf16[3584,2048]{1,0:T(8,128)(2,1)}) %all-gather.9.cloned.1.call-update) | async-done | bytes 14680080 | tf_op jit(solution)/shard_map/all_gather | solution.py:79
  274.0 15.3 %fusion.17 = f32[512,2048]{1,0:T(8,128)S(1)} fusion(bf16[3584,2048]{1,0:T(8,128)(2,1)} %all-gather.9.cloned.1.call-done, bf16[256,3584]{1,0:T(8,128)(2,1)} %collective-permute-done, bf16[256,3584]{1,0:T(8,128)(2,1)} %fusion.10, pred[]{:T(512)S(6)} %eq.3), kind=kOutput, calls=%fused_computation.43 | convolution fusion | flops 7532707840 | bytes 22544384 | tf_op jit(solution)/shard_map/dot_general | solution.py:84
  289.3 2.0 copy.22
  293.9 8.4 %fusion = (f32[4,2,512]{2,1,0:T(2,128)S(1)}, f32[4,1024,512,2]{2,1,3,0:T(8,128)}) fusion(pred[512,1024]{0,1:T(8,128)(4,1)S(1)} %copy-done.6, bf16[1024,4,256,1]{0,2,3,1:T(8,128)(2,1)S(1)} %bitcast.42, bf16[512,4,2,256]{3,0,2,1:T(8,128)(2,1)S(1)} %bitcast.43), kind=kOutput, calls=%fused_computation.1 | convolution fusion | flops 2155868160 | bytes 21512192 | tf_op jit(solution)/shard_map/cwap,bwp->wacb/dot_general | solution.py:48
  302.3 10.0 %fusion.7 = bf16[512,4,2,256]{0,3,2,1:T(8,128)(2,1)} fusion(bf16[1024,4,256,1]{0,2,3,1:T(8,128)(2,1)S(1)} %bitcast.41, f32[4,1024,512,2]{2,1,3,0:T(8,128)} %get-tuple-element.12, pred[512,1024]{0,1:T(8,128)(4,1)S(1)} %copy-done.6, f32[512,4,2]{0,2,1:T(2,128)S(1)} %bitcast.45), kind=kOutput, calls=%fused_computation.12 | convolution fusion | flops 2157969408 | bytes 21512192 | tf_op jit(solution)/shard_map/bpqu,ubm->qbpm/dot_general | solution.py:58
  312.3 75.4 %all-gather.11.cloned.1.call-done = bf16[2048,3584]{0,1:T(8,128)(2,1)} async-done(((bf16[2048,224]{0,1:T(8,128)(2,1)}), bf16[2048,3584]{0,1:T(8,128)(2,1)}) %all-gather.11.cloned.1.call-update) | async-done | bytes 14680080 | tf_op jit(solution)/shard_map/all_gather | solution.py:95
  387.7 11.7 %fusion.19 = bf16[512,3584]{1,0:T(8,128)(2,1)S(1)} fusion(bf16[512,2048]{0,1:T(8,128)(2,1)} %bitcast.44, bf16[2048,3584]{0,1:T(8,128)(2,1)} %all-gather.11.cloned.1.call-done), kind=kOutput, calls=%fused_computation.45 | convolution fusion | flops 7516192768 | bytes 20447232 | tf_op jit(solution)/shard_map/dot_general | solution.py:93
  399.4 1.8 copy-done.1
  404.0 41.0 %collective-permute-done.3 = bf16[256,3584]{1,0:T(8,128)(2,1)} collective-permute-done((bf16[256,3584]{1,0:T(8,128)(2,1)}, bf16[256,3584]{1,0:T(8,128)(2,1)}, u32[]{:S(2)}, u32[]{:S(2)}) %collective-permute-start.3) | collective-permute-done | bytes 1835040 | tf_op jit(solution)/shard_map/ppermute | solution.py:102
  445.0 2.7 multiply_reduce_fusion
  447.8 3.7 fusion.11
  (44 shorter events, 15.0 us)
Async XLA Ops:
  6.5 2.8 copy-start
  6.5 3.2 copy-start.7
  6.5 73.5 %all-gather.5.cloned.1.call-start = ((), (), s32[]{:S(2)}) async-start(), calls=%async_computation | async-start | bytes 7798784 | tf_op jit(solution)/shard_map/all_gather | solution.py:81
  7.3 145.3 %all-gather.7.cloned.1.call-start = ((), (), s32[]{:S(2)}) async-start(), calls=%async_computation.1 | async-start | bytes 7798784 | tf_op jit(solution)/shard_map/all_gather | solution.py:80
  8.0 266.0 %all-gather.9.cloned.1.call-start = ((), (), s32[]{:S(2)}) async-start(), calls=%async_computation.2 | async-start | bytes 15597568 | tf_op jit(solution)/shard_map/all_gather | solution.py:79
  8.7 378.9 %all-gather.11.cloned.1.call-start = ((), (), s32[]{:S(2)}) async-start(), calls=%async_computation.3 | async-start | bytes 15597568 | tf_op jit(solution)/shard_map/all_gather | solution.py:95
  11.5 43.3 %collective-permute-start = (bf16[256,3584]{1,0:T(8,128)(2,1)}, bf16[256,3584]{1,0:T(8,128)(2,1)}, u32[]{:S(2)}, u32[]{:S(2)}) collective-permute-start(bf16[256,3584]{1,0:T(8,128)(2,1)} %fusion.10), channel_id=1, source_target_pairs={{0,1},{1,0},{2,3},{3,2},{4,5},{5,4},{6,7},{7,6},{8,9},{9,8},{10,11... | collective-permute-start | bytes 5505032 | tf_op jit(solution)/shard_map/ppermute | solution.py:70
  90.4 84.8 %collective-permute-start.1 = (bf16[512,1024]{1,0:T(8,128)(2,1)}, bf16[512,1024]{1,0:T(8,128)(2,1)}, u32[]{:S(2)}, u32[]{:S(2)}) collective-permute-start(bf16[512,1024]{1,0:T(8,128)(2,1)} %convolution_convert_fusion), channel_id=1, source_target_pairs={{0,2},{2,4},{4,6},{6,8},{8,10},{10,12},{12,14},{14,16},{16,18},{18... | collective-permute-start | bytes 3145736 | tf_op jit(solution)/shard_map/ppermute | solution.py:13
  170.8 11.5 %collective-permute-start.2 = (bf16[512,1024]{0,1:T(8,128)(2,1)}, bf16[512,1024]{0,1:T(8,128)(2,1)}, u32[]{:S(2)}, u32[]{:S(2)}) collective-permute-start(bf16[512,1024]{0,1:T(8,128)(2,1)} %bitcast.39), channel_id=1, source_target_pairs={{0,2},{2,4},{4,6},{6,8},{8,10},{10,12},{12,14},{14,16},{16,18},{18... | collective-permute-start | bytes 3145736 | tf_op jit(solution)/shard_map/ppermute | solution.py:13
  175.2 7.1 %copy-start.3 = (bf16[512,4,256]{0,2,1:T(8,128)(2,1)S(1)}, bf16[512,4,256]{0,2,1:T(8,128)(2,1)}, u32[]{:S(2)}) copy-start(bf16[512,4,256]{0,2,1:T(8,128)(2,1)} %copy.11) | copy-start | bytes 3145732
  292.3 1.6 copy-start.5
  292.3 1.7 copy-start.6
  293.9 8.4 %copy-start.4 = (bf16[1024,1024]{0,1:T(8,128)(2,1)S(1)}, bf16[1024,1024]{0,1:T(8,128)(2,1)}, u32[]{:S(2)}) copy-start(bf16[1024,1024]{0,1:T(8,128)(2,1)} %copy.19) | copy-start | bytes 6291460
  399.4 1.8 copy-start.1
  401.2 46.6 %copy-start.8 = (f32[3584]{0:T(1024)S(1)}, f32[3584]{0:T(1024)}, u32[]{:S(2)}) copy-start(f32[3584]{0:T(1024)} %param.9) | copy-start | bytes 43012
  402.5 42.5 %collective-permute-start.3 = (bf16[256,3584]{1,0:T(8,128)(2,1)}, bf16[256,3584]{1,0:T(8,128)(2,1)}, u32[]{:S(2)}, u32[]{:S(2)}) collective-permute-start(bf16[256,3584]{1,0:T(8,128)(2,1)} %dynamic-slice_convert_fusion), channel_id=1, source_target_pairs={{0,1},{1,0},{2,3},{3,2},{4,5},{5,4},{6,7},{7,6},{8,9},{9,8},{10,11... | collective-permute-start | bytes 5505032 | tf_op jit(solution)/shard_map/ppermute | solution.py:102
  404.0 43.8 %copy-start.2 = (bf16[512,3584]{1,0:T(8,128)(2,1)S(1)}, bf16[512,3584]{1,0:T(8,128)(2,1)}, u32[]{:S(2)}) copy-start(bf16[512,3584]{1,0:T(8,128)(2,1)} %copy-done.1) | copy-start | bytes 11010052
Sparse Core Ops, SparseCore 0:
  9.6 70.3 all-gather.4
  82.3 70.1 all-gather.6
  154.8 119.1 all-gather.8
  276.1 111.4 all-gather.10
